TPU v7x, 8 devices: a whole 2x2x1 slice. The times are simulated.
8 devices in a mesh: dp: 1 (over z), tp: 8 (over y, x, core).
Axes of the slice: x: 2, y: 2, z: 1, core: 2. Of those that a mesh axis runs over, the one named last changes fastest.
Arguments:
- tokens: bfloat16 [1, 4096, 3584], P('dp', 'tp')
- start_pos: int32 [1], P('dp')
- cos_tab: float32 [1, 4096, 256], P('dp')
- sin_tab: float32 [1, 4096, 256], P('dp')
- key_cache: bfloat16 [2, 1, 4096, 8, 256], P(None, 'dp', None, 'tp')
- value_cache: bfloat16 [2, 1, 4096, 8, 256], P(None, 'dp', None, 'tp')
- slot_pos: int32 [1, 4096], P('dp')
- norm_params: bfloat16 [2, 4, 3584], replicated
- w_q: bfloat16 [2, 3584, 4096], P(None, None, 'tp')
- b_q: bfloat16 [2, 4096], P(None, 'tp')
- w_k: bfloat16 [2, 3584, 2048], P(None, None, 'tp')
- b_k: bfloat16 [2, 2048], P(None, 'tp')
- w_v: bfloat16 [2, 3584, 2048], P(None, None, 'tp')
- b_v: bfloat16 [2, 2048], P(None, 'tp')
- w_o: bfloat16 [2, 4096, 3584], P(None, 'tp')
- b_o: bfloat16 [2, 3584], replicated
- w_up: bfloat16 [2, 3584, 14336], P(None, None, 'tp')
- b_up: bfloat16 [2, 14336], P(None, 'tp')
- w_down: bfloat16 [2, 14336, 3584], P(None, 'tp')
- b_down: bfloat16 [2, 3584], replicated
Outputs:
- output 1: bfloat16 [1, 4096, 3584], P('dp', 'tp')
- output 2: bfloat16 [2, 1, 4096, 8, 256], P(None, 'dp', None, 'tp')
- output 3: bfloat16 [2, 1, 4096, 8, 256], P(None, 'dp', None, 'tp')
- output 4: int32 [1, 4096], P('dp')
All inputs are finite; a program needn't handle non-finite values.
Results may differ from a plain program's by a relative error of at most 0.0194662.
Values are sent between devices in bfloat16 or wider.
A program may use at most 1 GiB of HBM per device.

v0:
```python
import jax
import jax.numpy as jnp
from jax import lax
from jax.sharding import PartitionSpec as P

NORM_EPS = 1e-5


def layer_norm(hidden, gain, shift):
    values = hidden.astype(jnp.float32)
    centered = values - jnp.mean(values, axis=-1, keepdims=True)
    variance = jnp.mean(centered * centered, axis=-1, keepdims=True)
    scaled = centered * lax.rsqrt(variance + NORM_EPS)
    return (scaled * gain.astype(jnp.float32) + shift.astype(jnp.float32)).astype(jnp.bfloat16)


def apply_rotary(values, cos_b, sin_b):
    half = values.shape[-1] // 2
    turned = jnp.concatenate([-values[..., half:], values[..., :half]], axis=-1)
    return (values * cos_b + turned * sin_b).astype(jnp.bfloat16)


def write_chunk(cache, fresh, first_slot):
    window = cache.shape[0]
    length = fresh.shape[0]
    filler = jnp.zeros((window - length,) + fresh.shape[1:], fresh.dtype)
    placed = jnp.roll(jnp.concatenate([fresh, filler], axis=0), first_slot, axis=0)
    offset = (jnp.arange(window) - first_slot) % window
    keep = (offset >= length).reshape((window,) + (1,) * (cache.ndim - 1))
    return jnp.where(keep, cache, placed)


def project(acts, weight, bias):
    return jnp.einsum('bcm,mn->bcn', acts, weight, preferred_element_type=jnp.float32) + bias.astype(jnp.float32)


def local_attention(query, key_new, value_new, key_old, value_old, slot_pos, start_pos):
    chunk = query.shape[1]
    window = key_old.shape[1]
    scale = query.shape[-1] ** -0.5
    score_old = jnp.einsum('bckgd,bwkd->bkgcw', query, key_old, preferred_element_type=jnp.float32) * scale
    score_new = jnp.einsum('bckgd,bjkd->bkgcj', query, key_new, preferred_element_type=jnp.float32) * scale
    positions = start_pos[:, None] + jnp.arange(chunk)[None, :]
    held = slot_pos[:, None, :]
    old_ok = (held >= 0) & (held > positions[:, :, None] - window) & (held <= positions[:, :, None])
    new_ok = jnp.arange(chunk)[None, :] <= jnp.arange(chunk)[:, None]
    score_old = jnp.where(old_ok[:, None, None, :, :], score_old, -jnp.inf)
    score_new = jnp.where(new_ok, score_new, -jnp.inf)
    top = jnp.maximum(jnp.max(score_old, axis=-1, keepdims=True), jnp.max(score_new, axis=-1, keepdims=True))
    exp_old = jnp.exp(score_old - top)
    exp_new = jnp.exp(score_new - top)
    total = jnp.sum(exp_old, axis=-1) + jnp.sum(exp_new, axis=-1)
    mixed = jnp.einsum('bkgcw,bwkd->bckgd', exp_old.astype(jnp.bfloat16), value_old, preferred_element_type=jnp.float32)
    mixed = mixed + jnp.einsum('bkgcj,bjkd->bckgd', exp_new.astype(jnp.bfloat16), value_new, preferred_element_type=jnp.float32)
    return (mixed / jnp.transpose(total, (0, 3, 1, 2))[..., None]).astype(jnp.bfloat16)


def solution(mesh):
    row_spec = P('dp', 'tp', None)
    cache_spec = P(None, 'dp', None, 'tp', None)
    col_spec = P(None, None, 'tp')
    bias_spec = P(None, 'tp')
    in_specs = (row_spec, P('dp'), P('dp', None, None), P('dp', None, None), cache_spec, cache_spec, P('dp', None), P(), col_spec, bias_spec, col_spec, bias_spec, col_spec, bias_spec, P(None, 'tp', None), P(), col_spec, bias_spec, P(None, 'tp', None), P())
    out_specs = (row_spec, cache_spec, cache_spec, P('dp', None))

    def device_step(tokens, start_pos, cos_tab, sin_tab, key_cache, value_cache, slot_pos, norm_params, w_q, b_q, w_k, b_k, w_v, b_v, w_o, b_o, w_up, b_up, w_down, b_down):
        num_seqs = tokens.shape[0]
        chunk = cos_tab.shape[1]
        head_dim = cos_tab.shape[2]
        kv_local = w_k.shape[2] // head_dim
        group = w_q.shape[2] // w_k.shape[2]
        cos_b = cos_tab[:, :, None, :]
        sin_b = sin_tab[:, :, None, :]
        hidden = tokens
        fresh_keys = []
        fresh_values = []
        for layer in range(key_cache.shape[0]):
            normed = layer_norm(hidden, norm_params[layer, 0], norm_params[layer, 1])
            gathered = lax.all_gather(normed, 'tp', axis=1, tiled=True)
            query = apply_rotary(project(gathered, w_q[layer], b_q[layer]).reshape(num_seqs, chunk, kv_local * group, head_dim), cos_b, sin_b)
            key_new = apply_rotary(project(gathered, w_k[layer], b_k[layer]).reshape(num_seqs, chunk, kv_local, head_dim), cos_b, sin_b)
            value_new = project(gathered, w_v[layer], b_v[layer]).astype(jnp.bfloat16).reshape(num_seqs, chunk, kv_local, head_dim)
            mixed = local_attention(query.reshape(num_seqs, chunk, kv_local, group, head_dim), key_new, value_new, key_cache[layer], value_cache[layer], slot_pos, start_pos)
            part_sum = jnp.einsum('bcn,nm->bcm', mixed.reshape(num_seqs, chunk, -1), w_o[layer], preferred_element_type=jnp.float32).astype(jnp.bfloat16)
            summed = lax.psum_scatter(part_sum, 'tp', scatter_dimension=1, tiled=True)
            middle = (hidden.astype(jnp.float32) + summed.astype(jnp.float32) + b_o[layer].astype(jnp.float32)).astype(jnp.bfloat16)
            normed = layer_norm(middle, norm_params[layer, 2], norm_params[layer, 3])
            gathered = lax.all_gather(normed, 'tp', axis=1, tiled=True)
            active = jax.nn.gelu(project(gathered, w_up[layer], b_up[layer]), approximate=True).astype(jnp.bfloat16)
            part_sum = jnp.einsum('bcf,fm->bcm', active, w_down[layer], preferred_element_type=jnp.float32).astype(jnp.bfloat16)
            summed = lax.psum_scatter(part_sum, 'tp', scatter_dimension=1, tiled=True)
            hidden = (middle.astype(jnp.float32) + summed.astype(jnp.float32) + b_down[layer].astype(jnp.float32)).astype(jnp.bfloat16)
            fresh_keys.append(key_new)
            fresh_values.append(value_new)
        first_slot = start_pos % key_cache.shape[2]
        write_all = jax.vmap(jax.vmap(write_chunk), in_axes=(0, 0, None))
        key_out = write_all(key_cache, jnp.stack(fresh_keys), first_slot)
        value_out = write_all(value_cache, jnp.stack(fresh_values), first_slot)
        positions = start_pos[:, None] + jnp.arange(chunk)[None, :]
        pos_out = jax.vmap(write_chunk)(slot_pos, positions, first_slot)
        return hidden, key_out, value_out, pos_out

    return jax.shard_map(device_step, mesh=mesh, in_specs=in_specs, out_specs=out_specs, check_vma=False)
```

profile of v0, /device:TPU:0, one launch (start us, length us, event | category | flops | bytes accessed | tf_op | source)
XLA Modules:
  0.0 2369.4 jit_solution(143611518571472246)
XLA Ops:
  7.2 2.7 convert_reduce_fusion.3
  10.0 3.1 fusion.102
  13.1 0.9 convert_reduce_fusion.6
  14.0 3.8 fusion.105
  18.8 5.7 copy.24
  24.5 5.6 copy.25
  30.1 6.4 copy.31
  38.4 11.0 iota_compare_fusion
  49.4 21.8 compare_and_fusion
  71.2 87.1 %all-gather.5.cloned.1.call-done = bf16[1,4096,3584]{2,1,0:T(8,128)(2,1)} async-done(((bf16[1,512,3584]{2,1,0:T(8,128)(2,1)}), bf16[1,4096,3584]{2,1,0:T(8,128)(2,1)}) %all-gather.5.cloned.1.call-update) | async-done | bytes 29360144 | tf_op jit(solution)/shard_map/all_gather | solution.py:79
  158.3 14.1 fusion.124
  172.4 3.1 fusion.184
  176.2 20.2 fusion.114
  196.4 2.8 fusion.151
  199.2 2.8 copy-done.6
  202.0 6.0 maximum_multiply_fusion
  208.0 11.3 fusion.85
  219.3 55.2 %fusion.8 = (f32[2,4096]{1,0:T(2,128)S(1)}, f32[4096,2,4096]{0,2,1:T(8,128)}) fusion(pred[4096,4096]{0,1:T(8,128)(4,1)} %compare_and_fusion, bf16[4096,2,256]{0,2,1:T(8,128)(2,1)} %bitcast.383, bf16[2,1,4096,1,256]{4,2,3,1,0:T(8,128)(2,1)} %param.26), kind=kOutput, calls=%fused_computation.16 | convolution fusion | flops 17280524288 | bytes 157319168 | tf_op jit(solution)/shard_map/bckgd,bwkd->bkgcw/dot_general | solution.py:41
  274.5 60.1 %fusion.9 = (f32[2,4096]{1,0:T(2,128)S(1)}, f32[4096,4096,2]{1,0,2:T(8,128)}) fusion(pred[4096,4096]{0,1:T(8,128)(4,1)} %iota_compare_fusion, bf16[4096,2,256]{0,2,1:T(8,128)(2,1)} %bitcast.384, f32[1,4096,256]{1,2,0:T(8,128)} %copy.25, f32[1,4096,128]{1,2,0:T(8,128)S(1)} %get-tuple-element.67, f32[1,4096,128]{1,2,0:T(8,128)} %get-tuple-element.68, ...), kind=kOutput, calls=%fused_computation.17 | convolution fusion | flops 17285767168 | bytes 171999232 | tf_op jit(solution)/shard_map/bckgd,bjkd->bkgcj/dot_general | solution.py:42
  334.6 92.0 %fusion.2 = (f32[2,4096]{1,0:T(2,128)S(1)}, f32[2,4096]{1,0:T(2,128)S(1)}) fusion(f32[4096,4096,2]{1,0,2:T(8,128)} %get-tuple-element.80, f32[2,4096]{1,0:T(2,128)S(1)} %max.16, pred[4096,4096]{0,1:T(8,128)(4,1)} %iota_compare_fusion, f32[4096,2,4096]{0,2,1:T(8,128)} %get-tuple-element.78, pred[4096,4096]{0,1:T(8,128)(4,1)} %compare_and_fusion), kind=kLoop, calls=%fused_computation.10 | loop fusion | flops 268419072 | bytes 302088192 | tf_op jit(solution)/shard_map/reduce_sum | solution.py:52
  426.6 14.1 fusion.139
  440.8 56.4 %fusion.18 = f32[256,2,4096]{2,0,1:T(8,128)} fusion(f32[4096,4096,2]{1,0,2:T(8,128)} %get-tuple-element.80, f32[2,4096]{1,0:T(2,128)S(1)} %max.16, pred[4096,4096]{0,1:T(8,128)(4,1)} %iota_compare_fusion, bf16[4096,256]{0,1:T(8,128)(2,1)S(1)} %fusion.139), kind=kOutput, calls=%fused_computation.26 | convolution fusion | flops 17314086912 | bytes 161513472 | tf_op jit(solution)/shard_map/bkgcj,bjkd->bckgd/dot_general | solution.py:54
  497.2 55.4 %fusion.89 = bf16[1,4096,1,2,256]{1,4,3,2,0:T(8,128)(2,1)} fusion(f32[256,2,4096]{2,0,1:T(8,128)} %fusion.18, f32[4096,2,4096]{0,2,1:T(8,128)} %get-tuple-element.78, f32[2,4096]{1,0:T(2,128)S(1)} %max.16, pred[4096,4096]{0,1:T(8,128)(4,1)} %compare_and_fusion, f32[4096,2]{0,1:T(2,128)S(1)} %add_bitcast_fusion.1, bf16[2,1,4096,1,256]{2,4,3,1,0:T(8,128)(2,1)} %copy.31), kind=kOutput, calls=%fused_computation.123 | convolution fusion | flops 17320378368 | bytes 165740544 | tf_op jit(solution)/shard_map/bkgcw,bwkd->bckgd/dot_general | solution.py:53
  552.7 22.4 fusion.60
  576.4 164.9 %reduce-scatter.5.cloned.1.call-done = bf16[1,512,3584]{2,1,0:T(8,128)(2,1)} async-done(((bf16[1,4096,3584]{2,1,0:T(8,128)(2,1)}), bf16[1,512,3584]{2,1,0:T(8,128)(2,1)}) %reduce-scatter.5.cloned.1.call-update) | async-done | bytes 3670032 | tf_op jit(solution)/shard_map/reduce_scatter | solution.py:85
  741.3 4.8 convert_reduce_fusion.2
  746.2 1.1 fusion.98
  748.0 3.8 fusion.101
  752.9 136.5 %all-gather.7.cloned.1.call-done = bf16[1,4096,3584]{2,1,0:T(8,128)(2,1)} async-done(((bf16[1,512,3584]{2,1,0:T(8,128)(2,1)}), bf16[1,4096,3584]{2,1,0:T(8,128)(2,1)}) %all-gather.7.cloned.1.call-update) | async-done | bytes 29360144 | tf_op jit(solution)/shard_map/all_gather | solution.py:88
  889.4 66.0 %fusion.35 = bf16[4096,1792]{1,0:T(8,128)(2,1)} fusion(bf16[1,4096,3584]{2,1,0:T(8,128)(2,1)} %all-gather.7.cloned.1.call-done, f32[1792]{0:T(1024)S(1)} %get-tuple-element.48, bf16[2,3584,1792]{2,1,0:T(8,128)(2,1)} %param.38), kind=kOutput, calls=%fused_computation.47 | convolution fusion | flops 52686749696 | bytes 56892416 | tf_op jit(solution)/shard_map/bcm,mn->bcn/dot_general | solution.py:34
  955.4 61.4 %fusion.62 = bf16[1,4096,3584]{2,1,0:T(8,128)(2,1)} fusion(bf16[4096,1792]{1,0:T(8,128)(2,1)} %fusion.35, bf16[2,1792,3584]{2,1,0:T(8,128)(2,1)} %param.40), kind=kOutput, calls=%fused_computation.74 | convolution fusion | flops 52628029440 | bytes 56885248 | tf_op jit(solution)/shard_map/bcf,fm->bcm/dot_general | solution.py:90
  1018.1 165.0 %reduce-scatter.7.cloned.1.call-done = bf16[1,512,3584]{2,1,0:T(8,128)(2,1)} async-done(((bf16[1,4096,3584]{2,1,0:T(8,128)(2,1)}), bf16[1,512,3584]{2,1,0:T(8,128)(2,1)}) %reduce-scatter.7.cloned.1.call-update) | async-done | bytes 3670032 | tf_op jit(solution)/shard_map/reduce_scatter | solution.py:91
  1183.1 4.8 convert_reduce_fusion.1
  1188.0 1.1 fusion.94
  1189.8 3.8 fusion.97
  1193.9 137.3 %all-gather.9.cloned.1.call-done = bf16[1,4096,3584]{2,1,0:T(8,128)(2,1)} async-done(((bf16[1,512,3584]{2,1,0:T(8,128)(2,1)}), bf16[1,4096,3584]{2,1,0:T(8,128)(2,1)}) %all-gather.9.cloned.1.call-update) | async-done | bytes 29360144 | tf_op jit(solution)/shard_map/all_gather | solution.py:79
  1331.2 14.1 fusion.130
  1345.4 3.3 fusion.186
  1349.3 20.1 fusion.117
  1369.5 2.8 fusion.150
  1372.3 2.8 copy-done.7
  1375.0 5.5 maximum_multiply_fusion.1
  1380.5 11.3 fusion.87
  1391.8 55.6 %fusion.10 = (f32[2,4096]{1,0:T(2,128)S(1)}, f32[4096,2,4096]{0,2,1:T(8,128)}) fusion(pred[4096,4096]{0,1:T(8,128)(4,1)} %compare_and_fusion, bf16[4096,2,256]{0,2,1:T(8,128)(2,1)} %bitcast.385, bf16[2,1,4096,1,256]{4,2,3,1,0:T(8,128)(2,1)} %param.26), kind=kOutput, calls=%fused_computation.18 | convolution fusion | flops 17280524288 | bytes 157319168 | tf_op jit(solution)/shard_map/bckgd,bwkd->bkgcw/dot_general | solution.py:41
  1447.4 60.1 %fusion.11 = (f32[2,4096]{1,0:T(2,128)S(1)}, f32[4096,4096,2]{1,0,2:T(8,128)}) fusion(pred[4096,4096]{0,1:T(8,128)(4,1)} %iota_compare_fusion, bf16[4096,2,256]{0,2,1:T(8,128)(2,1)} %bitcast.386, f32[1,4096,256]{1,2,0:T(8,128)} %copy.25, f32[1,4096,128]{1,2,0:T(8,128)S(1)} %get-tuple-element.63, f32[1,4096,128]{1,2,0:T(8,128)} %get-tuple-element.64, ...), kind=kOutput, calls=%fused_computation.19 | convolution fusion | flops 17285767168 | bytes 171999232 | tf_op jit(solution)/shard_map/bckgd,bjkd->bkgcj/dot_general | solution.py:42
  1507.6 91.9 %fusion.6 = (f32[2,4096]{1,0:T(2,128)S(1)}, f32[2,4096]{1,0:T(2,128)S(1)}) fusion(f32[4096,4096,2]{1,0,2:T(8,128)} %get-tuple-element.84, f32[2,4096]{1,0:T(2,128)S(1)} %max.17, pred[4096,4096]{0,1:T(8,128)(4,1)} %iota_compare_fusion, f32[4096,2,4096]{0,2,1:T(8,128)} %get-tuple-element.82, pred[4096,4096]{0,1:T(8,128)(4,1)} %compare_and_fusion), kind=kLoop, calls=%fused_computation.14 | loop fusion | flops 268419072 | bytes 302088192 | tf_op jit(solution)/shard_map/reduce_sum | solution.py:52
  1599.4 14.3 fusion.136
  1613.8 56.4 %fusion.22 = f32[256,2,4096]{2,0,1:T(8,128)} fusion(f32[4096,4096,2]{1,0,2:T(8,128)} %get-tuple-element.84, f32[2,4096]{1,0:T(2,128)S(1)} %max.17, pred[4096,4096]{0,1:T(8,128)(4,1)} %iota_compare_fusion, bf16[4096,256]{0,1:T(8,128)(2,1)S(1)} %fusion.136), kind=kOutput, calls=%fused_computation.28 | convolution fusion | flops 17314086912 | bytes 161513472 | tf_op jit(solution)/shard_map/bkgcj,bjkd->bckgd/dot_general | solution.py:54
  1670.2 55.1 %fusion.88 = bf16[1,4096,1,2,256]{1,4,3,2,0:T(8,128)(2,1)} fusion(f32[256,2,4096]{2,0,1:T(8,128)} %fusion.22, f32[4096,2,4096]{0,2,1:T(8,128)} %get-tuple-element.82, f32[2,4096]{1,0:T(2,128)S(1)} %max.17, pred[4096,4096]{0,1:T(8,128)(4,1)} %compare_and_fusion, f32[4096,2]{0,1:T(2,128)S(1)} %add_bitcast_fusion, bf16[2,1,4096,1,256]{2,4,3,1,0:T(8,128)(2,1)} %copy.31), kind=kOutput, calls=%fused_computation.121 | convolution fusion | flops 17320378368 | bytes 165740544 | tf_op jit(solution)/shard_map/bkgcw,bwkd->bckgd/dot_general | solution.py:53
  1725.3 22.6 fusion.61
  1747.9 166.2 %reduce-scatter.9.cloned.1.call-done = bf16[1,512,3584]{2,1,0:T(8,128)(2,1)} async-done(((bf16[1,4096,3584]{2,1,0:T(8,128)(2,1)}), bf16[1,512,3584]{2,1,0:T(8,128)(2,1)}) %reduce-scatter.9.cloned.1.call-update) | async-done | bytes 3670032 | tf_op jit(solution)/shard_map/reduce_scatter | solution.py:85
  1914.1 4.8 convert_reduce_fusion
  1919.0 1.1 fusion.90
  1920.8 3.8 fusion.93
  1924.6 137.5 %all-gather.11.cloned.1.call-done = bf16[1,4096,3584]{2,1,0:T(8,128)(2,1)} async-done(((bf16[1,512,3584]{2,1,0:T(8,128)(2,1)}), bf16[1,4096,3584]{2,1,0:T(8,128)(2,1)}) %all-gather.11.cloned.1.call-update) | async-done | bytes 29360144 | tf_op jit(solution)/shard_map/all_gather | solution.py:88
  2062.2 66.4 %fusion.43 = bf16[4096,1792]{1,0:T(8,128)(2,1)} fusion(bf16[1,4096,3584]{2,1,0:T(8,128)(2,1)} %all-gather.11.cloned.1.call-done, f32[1792]{0:T(1024)S(1)} %copy-done.30, bf16[2,3584,1792]{2,1,0:T(8,128)(2,1)} %param.38), kind=kOutput, calls=%fused_computation.55 | convolution fusion | flops 52686749696 | bytes 56892416 | tf_op jit(solution)/shard_map/bcm,mn->bcn/dot_general | solution.py:34
  2128.6 61.4 %fusion.63 = bf16[1,4096,3584]{2,1,0:T(8,128)(2,1)} fusion(bf16[4096,1792]{1,0:T(8,128)(2,1)} %fusion.43, bf16[2,1792,3584]{2,1,0:T(8,128)(2,1)} %param.40), kind=kOutput, calls=%fused_computation.75 | convolution fusion | flops 52628029440 | bytes 56885248 | tf_op jit(solution)/shard_map/bcf,fm->bcm/dot_general | solution.py:90
  2190.0 6.5 copy.44
  2197.4 9.4 fusion.168
  2207.5 13.2 fusion.144
  2220.7 6.3 copy.47
  2227.0 6.3 copy.46
  2233.3 123.0 %reduce-scatter.11.cloned.1.call-done = bf16[1,512,3584]{2,1,0:T(8,128)(2,1)} async-done(((bf16[1,4096,3584]{2,1,0:T(8,128)(2,1)}), bf16[1,512,3584]{2,1,0:T(8,128)(2,1)}) %reduce-scatter.11.cloned.1.call-update) | async-done | bytes 3670032 | tf_op jit(solution)/shard_map/reduce_scatter | solution.py:91
  2356.3 6.1 fusion.113
  (111 shorter events, 11.6 us)
Async XLA Ops:
  7.2 6.0 copy-start.15
  7.2 151.1 %all-gather.5.cloned.1.call-start = ((), (), s32[]{:S(2)}) async-start(), calls=%async_computation.4 | async-start | bytes 33030144 | tf_op jit(solution)/shard_map/all_gather | solution.py:79
  7.2 6.8 copy-start.4
  17.8 723.5 %reduce-scatter.5.cloned.1.call-start = ((), (), s32[]{:S(2)}) async-start(), calls=%async_computation.5 | async-start | bytes 33030144 | tf_op jit(solution)/shard_map/reduce_scatter | solution.py:85
  24.5 12.1 copy-start.31
  24.5 12.7 copy-start.32
  24.5 13.3 copy-start.29
  24.5 13.9 copy-start.16
  172.4 3.8 copy-start.8
  196.4 5.6 copy-start.6
  196.4 5.6 copy-start
  334.6 92.0 %copy-start.36 = (f32[1,256]{1,0:T(1,128)S(1)}, f32[1,256]{1,0:T(1,128)}, u32[]{:S(2)}) copy-start(f32[1,256]{1,0:T(1,128)} %get-tuple-element.74) | copy-start | bytes 3076
  440.8 56.4 %copy-start.13 = (bf16[4096,256]{0,1:T(8,128)(2,1)}, bf16[4096,256]{0,1:T(8,128)(2,1)S(1)}, u32[]{:S(2)}) copy-start(bf16[4096,256]{0,1:T(8,128)(2,1)S(1)} %fusion.139) | copy-start | bytes 6291460
  575.0 0.7 copy-start.26
  575.1 314.3 %all-gather.7.cloned.1.call-start = ((), (), s32[]{:S(2)}) async-start(), calls=%async_computation.6 | async-start | bytes 33030144 | tf_op jit(solution)/shard_map/all_gather | solution.py:88
  741.3 6.7 copy-start.24
  741.3 6.7 copy-start.25
  746.2 1.8 copy-start.3
  746.2 6.1 copy-start.28
  751.8 431.3 %reduce-scatter.7.cloned.1.call-start = ((), (), s32[]{:S(2)}) async-start(), calls=%async_computation.7 | async-start | bytes 33030144 | tf_op jit(solution)/shard_map/reduce_scatter | solution.py:91
  1016.8 0.7 copy-start.27
  1016.8 314.4 %all-gather.9.cloned.1.call-start = ((), (), s32[]{:S(2)}) async-start(), calls=%async_computation.8 | async-start | bytes 33030144 | tf_op jit(solution)/shard_map/all_gather | solution.py:79
  1183.1 6.7 copy-start.22
  1183.1 6.7 copy-start.23
  1187.9 1.9 copy-start.2
  1187.9 143.2 %copy-start.35 = (f32[1,256]{1,0:T(1,128)S(1)}, f32[1,256]{1,0:T(1,128)}, u32[]{:S(2)}) copy-start(f32[1,256]{1,0:T(1,128)} %get-tuple-element.75) | copy-start | bytes 3076
  1193.6 720.5 %reduce-scatter.9.cloned.1.call-start = ((), (), s32[]{:S(2)}) async-start(), calls=%async_computation.9 | async-start | bytes 33030144 | tf_op jit(solution)/shard_map/reduce_scatter | solution.py:85
  1345.3 3.9 copy-start.9
  1345.3 3.9 copy-start.33
  1369.4 5.6 copy-start.7
  1369.5 5.6 copy-start.1
  1507.5 91.9 %copy-start.34 = (f32[1,256]{1,0:T(1,128)S(1)}, f32[1,256]{1,0:T(1,128)}, u32[]{:S(2)}) copy-start(f32[1,256]{1,0:T(1,128)} %get-tuple-element.73) | copy-start | bytes 3076
  1613.8 56.4 %copy-start.14 = (bf16[4096,256]{0,1:T(8,128)(2,1)}, bf16[4096,256]{0,1:T(8,128)(2,1)S(1)}, u32[]{:S(2)}) copy-start(bf16[4096,256]{0,1:T(8,128)(2,1)S(1)} %fusion.136) | copy-start | bytes 6291460
  1747.8 166.3 %copy-start.19 = (f32[3584]{0:T(1024)S(1)}, f32[3584]{0:T(1024)}, u32[]{:S(2)}) copy-start(f32[3584]{0:T(1024)} %get-tuple-element.45) | copy-start | bytes 43012
  1747.9 314.3 %all-gather.11.cloned.1.call-start = ((), (), s32[]{:S(2)}) async-start(), calls=%async_computation.10 | async-start | bytes 33030144 | tf_op jit(solution)/shard_map/all_gather | solution.py:88
  1914.1 6.7 copy-start.20
  1914.1 6.7 copy-start.21
  1919.0 1.8 copy-start.5
  1919.0 143.2 %copy-start.30 = (f32[1792]{0:T(1024)S(1)}, f32[1792]{0:T(1024)}, u32[]{:S(2)}) copy-start(f32[1792]{0:T(1024)} %get-tuple-element.47) | copy-start | bytes 21508
  1924.6 431.7 %reduce-scatter.11.cloned.1.call-start = ((), (), s32[]{:S(2)}) async-start(), calls=%async_computation.11 | async-start | bytes 33030144 | tf_op jit(solution)/shard_map/reduce_scatter | solution.py:91
  2190.0 6.6 copy-start.17
  2190.0 7.4 copy-start.12
  2197.4 9.4 copy-start.10
  2197.4 10.1 copy-start.11
  2220.6 135.7 %copy-start.18 = (f32[3584]{0:T(1024)S(1)}, f32[3584]{0:T(1024)}, u32[]{:S(2)}) copy-start(f32[3584]{0:T(1024)} %get-tuple-element.43) | copy-start | bytes 43012
Sparse Core Ops, SparseCore 0:
  18.0 140.2 all-gather.4
  575.2 166.1 reduce-scatter.4
  751.9 137.4 all-gather.6
  1016.9 166.1 reduce-scatter.6
  1193.7 137.4 all-gather.8
  1748.0 166.0 reduce-scatter.8
  1924.7 137.4 all-gather.10
  2190.1 166.1 reduce-scatter.10
where the time goes:
time: 2370 us
  waiting for transfers between devices  1120 us (47%)
  matrix products  851 us (36%)
  other arithmetic  336 us (14%)
  local copies, waits for them, and re-layouts  47.7 us (2%)
    reduce_scatter x4, waiting for transfers between devices, device_step(): summed = lax.psum_scatter(part_sum, 'tp', scatter_dimension=1, tiled=True)  619 us
    all_gather x4, waiting for transfers between devices, device_step(): gathered = lax.all_gather(normed, 'tp', axis=1, tiled=True)  498 us
    dot_general x8, matrix products, project(): jnp.einsum('bcm,mn->bcn', acts, weight, preferred_element_type=jnp.float32)  229 us
    reduce_sum x2, other arithmetic, local_attention(): total = jnp.sum(exp_old, axis=-1) + jnp.sum(exp_new, axis=-1)  184 us
    dot_general x2, matrix products, device_step(): jnp.einsum('bcf,fm->bcm', active, w_down[layer], preferred_element_type=j...  123 us
    dot_general x2, matrix products, local_attention(): jnp.einsum('bckgd,bjkd->bkgcj', query, key_new, preferred_element_type=jn...  120 us
    dot_general x2, matrix products, local_attention(): jnp.einsum('bkgcj,bjkd->bckgd', exp_new.astype(jnp.bfloat16), value_new,...  113 us
    dot_general x2, matrix products, local_attention(): jnp.einsum('bckgd,bwkd->bkgcw', query, key_old, preferred_element_type=jn...  111 us
  transfers between devices with their start and end apart: 8, of which 8 were waited for; matrix products, arithmetic and copies ran while one was open for 4% of the time, Pallas kernels for 0%

commit v1 on v0

v1 whole, which is shorter than its diff:
```python
import functools

import jax
import jax.numpy as jnp
from jax import lax
from jax.experimental import pallas as pl
from jax.experimental.pallas import tpu as pltpu
from jax.sharding import PartitionSpec as P

NORM_EPS = 1e-5
LOG2E = 1.4426950408889634
CHUNKS = 4
KEY_TILE = 512
LANES = 128
WIDE = 512
ROW_BLOCK = 16
PAIR = 2
GROUP = 4
WEIGHT_SLOTS = 3
SLOTS = 5
ROLL_ROWS = 256
ROLL_SLOTS = 4
EARLY = 2
LOWEST = -3.3e38
VMEM_LIMIT = 67_043_328
BF16 = jnp.bfloat16
F32 = jnp.float32
MESH = pl.DeviceIdType.MESH

ANY = pl.BlockSpec(memory_space=pl.ANY)
SMEM = pl.BlockSpec(memory_space=pltpu.SMEM)
VMEM = pl.BlockSpec(memory_space=pltpu.VMEM)
DMA = pltpu.SemaphoreType.DMA


def vm(*shape, dtype=BF16):
    return pltpu.VMEM(shape, dtype)


def dma(*shape):
    return DMA(shape) if shape else DMA


def whole(ref, sem):
    pltpu.make_async_copy(ref, ref, sem).wait()


def one_row(ref, n):
    return ref[pl.ds(n, 1), :].astype(F32)


def gelu_tanh(x):
    inner = 0.7978845608028654 * (x + 0.044715 * (x * x * x))
    return 0.5 * x * (1.0 + jnp.tanh(inner))


def normalized(values, gain, shift):
    centered = values - jnp.mean(values, axis=-1, keepdims=True)
    variance = jnp.mean(centered * centered, axis=-1, keepdims=True)
    return (centered * lax.rsqrt(variance + NORM_EPS) * gain + shift).astype(BF16)


def rotate(planes, put, window, shift, first, last):
    def tile(n, carry):
        want = lax.broadcasted_iota(jnp.int32, (ROLL_ROWS, 1), 0) + (n * ROLL_ROWS + shift)
        want = jnp.where(want >= window, want - window, want)
        pick = jnp.where(lax.broadcasted_iota(jnp.int32, (1, window), 1) == want, 1.0, 0.0).astype(BF16)
        put(n, [jnp.dot(pick, plane(), preferred_element_type=F32).astype(BF16) for plane in planes])
        return carry

    lax.fori_loop(first, last, tile, 0)


def reset_state(st_s, w):
    for g in range(PAIR):
        st_s[w, g, :, 0:LANES] = jnp.full((st_s.shape[2], LANES), LOWEST, F32)
        st_s[w, g, :, LANES:] = jnp.zeros((st_s.shape[2], st_s.shape[3] - LANES), F32)


def flash_step(st_s, w, s_s, scale, mask, values, next_scores):
    for g in range(PAIR):
        s = jnp.where(mask, s_s[g] * scale, -jnp.inf)
        s_next = next_scores(g)
        m_prev = st_s[w, g, :, 0:LANES]
        m_next = jnp.maximum(m_prev, jnp.max(s, axis=1, keepdims=True))
        e = jnp.exp2(s - jnp.concatenate([m_next] * (s.shape[1] // LANES), axis=1))
        alpha = jnp.exp2(m_prev - m_next)
        total = st_s[w, g, :, LANES:2 * LANES] * alpha
        for k in range(s.shape[1] // LANES):
            total = total + e[:, k * LANES:(k + 1) * LANES]
        st_s[w, g, :, LANES:2 * LANES] = total
        st_s[w, g, :, 0:LANES] = m_next
        mixed = jnp.dot(e.astype(BF16), values(g), preferred_element_type=F32)
        st_s[w, g, :, 2 * LANES:] = st_s[w, g, :, 2 * LANES:] * jnp.concatenate([alpha] * (mixed.shape[1] // LANES), axis=1) + mixed
        s_s[g] = s_next


def score_tile(queries, keys):
    return lax.dot_general(queries, keys, (((1,), (1,)), ((), ())), preferred_element_type=F32)


class Place:
    def __init__(self):
        me = lax.axis_index('tp')
        self.core = lax.rem(me, 2)
        self.xb = lax.rem(lax.div(me, 2), 2)
        self.yb = lax.div(me, 4)
        self.peer = me + 1 - 2 * self.core
        self.x = me + 2 - 4 * self.xb
        self.y = me + 4 - 8 * self.yb

    def member(self, i):
        xb = self.xb + lax.rem(i, 2) * (1 - 2 * self.xb)
        yb = self.yb + lax.div(i, 2) * (1 - 2 * self.yb)
        return yb * 2 + xb

    def barrier(self, others):
        sem = pltpu.get_barrier_semaphore()
        for other in others:
            pl.semaphore_signal(sem, inc=1, device_id={'tp': other}, device_id_type=MESH)
        pl.semaphore_wait(sem, len(others))


def remote(src, dst, send_sem, recv_sem, other):
    return pltpu.make_async_remote_copy(src_ref=src, dst_ref=dst, send_sem=send_sem, recv_sem=recv_sem, device_id={'tp': other}, device_id_type=MESH)


class Gather:
    def __init__(self, place, x_s, slot, send, recv, rows):
        self.place, self.x_s, self.slot, self.send, self.recv, self.rows = place, x_s, slot, send, recv, rows

    def copy(self, c, kind):
        r, h = self.rows, self.rows // 2
        src, dst, size, other = ((0, r, r, self.place.x), (0, 2 * r, r, self.place.y), (r, 3 * r, h, self.place.y), (2 * r + h, 3 * r + h, h, self.place.x))[kind]
        slot = self.slot(c)
        return remote(self.x_s.at[slot, pl.ds(src, size)], self.x_s.at[slot, pl.ds(dst, size)], self.send.at[c, kind], self.recv.at[c, kind], other)

    def start(self, c):
        self.copy(c, 0).start()
        self.copy(c, 1).start()

    def forward(self, c):
        self.copy(c, 0).wait_recv()
        self.copy(c, 2).start()
        self.copy(c, 1).wait_recv()
        self.copy(c, 3).start()

    def finish(self, c):
        self.copy(c, 2).wait_recv()
        self.copy(c, 3).wait_recv()

    def drain(self, c):
        for kind in range(GROUP):
            self.copy(c, kind).wait_send()


class Scatter:
    def __init__(self, place, out_s, slot, land_s, send, recv, rows):
        self.place, self.out_s, self.slot, self.land_s, self.send, self.recv, self.rows = place, out_s, slot, land_s, send, recv, rows

    def copy(self, c, kind):
        r, h = self.rows, self.rows // 2
        x, y = self.place.x, self.place.y
        src, dst, other = ((3 * r, 2 * r, x), (3 * r + h, 2 * r + h, y), (r, 0, x), (2 * r + h, r + h, y), (r + h, h, x), (2 * r, r, y))[kind]
        return remote(self.out_s.at[self.slot(c), pl.ds(src, h)], self.land_s.at[c, pl.ds(dst, h)], self.send.at[c, kind], self.recv.at[c, kind], other)

    def start(self, c):
        for kind in range(GROUP):
            self.copy(c, kind).start()

    def relay(self, c, settled):
        r, h = self.rows, self.rows // 2
        slot = self.slot(c)
        for kind, src, dst in ((0, 2 * r, 2 * r), (1, 2 * r + h, r + h)):
            self.copy(c, kind).wait_recv()

            def block(n, carry):
                at = pl.multiple_of(n * ROW_BLOCK, ROW_BLOCK)
                mine = self.out_s[slot, pl.ds(dst + at, ROW_BLOCK), :].astype(F32)
                came = self.land_s[c, pl.ds(src + at, ROW_BLOCK), :].astype(F32)
                self.out_s[slot, pl.ds(dst + at, ROW_BLOCK), :] = (mine + came).astype(BF16)
                return carry

            lax.fori_loop(0, h // ROW_BLOCK, block, 0)

        @pl.when(settled >= 0)
        def _():
            self.drain(settled)

        self.copy(c, 5).start()
        self.copy(c, 4).start()

    def finish(self, c):
        for kind in range(2, 6):
            self.copy(c, kind).wait_recv()

    def drain(self, c):
        for kind in range(6):
            self.copy(c, kind).wait_send()

    def total(self, c, at):
        own = self.out_s[self.slot(c), pl.ds(at, ROW_BLOCK), :].astype(F32)
        came = [self.land_s[c, pl.ds(k * self.rows + at, ROW_BLOCK), :].astype(F32) for k in range(PAIR)]
        return own + came[0] + came[1]


def step_kernel(dims, scal, *refs):
    layers, chunks, rows, model, hd, window, ffn = dims
    (tokens, norms, cos, sin, wq, wk, wv, bq, bk, bv, bu, bq_push, bk_push, bv_push, bu_push, kc, vc, wo, up, down, b_o, b_down,
     h_out, kv_rolled, q_hbm, state, qkv_peer, wo_peer, up_peer, down_peer,
     big_s, q_s, t_s, s_s, wo_s, xo_s, land_s, mid_s, st_s, ba_s, bm_s, bq_s, bk_s, bv_s, bu_s,
     a1_send, a1_recv, a2_send, a2_recv, r1_send, r1_recv, r2_send, r2_recv, old_send, old_recv, kv_send, kv_recv, p_send, p_recv, b_send, b_recv,
     h_sem, t_sem, raw_sem, wa_sem, wo_sem, wm_sem, q_sem, st_sem, f_sem, ready) = refs
    place = Place()
    start_pos = scal[0]
    first_slot = lax.rem(start_pos, window)
    floor = window - 1 - start_pos
    block = rows * chunks
    tall = PAIR * rows
    tile = KEY_TILE
    tiles = window // tile
    scale = LOG2E * hd ** -0.5
    deep = GROUP * hd
    q_rows = PAIR * GROUP * tall
    last_chunk = chunks - 1
    roll_tiles = window // ROLL_ROWS

    def here(rows_from, count):
        return pl.ds(pl.multiple_of(rows_from, rows), count)

    def position(c, i):
        return (place.member(i) * PAIR + place.core) * block + c * rows

    def region(g, new):
        return jnp.where(new, (3 - g) * window, g * window)

    def q_row(c, g, i):
        return ((lax.rem(c, PAIR) * PAIR + g) * GROUP + i) * tall

    def tile_of(g, new, at, kv):
        return big_s[pl.ds(pl.multiple_of(region(g, new) + at, tile), tile), kv * hd:(kv + 1) * hd]

    def scores(c, i, g, new, at):
        return score_tile(q_s[here(q_row(c, g, i), tall), :], tile_of(g, new, at, 0))

    def row_blocks(body):
        def one(n, carry):
            body(pl.ds(pl.multiple_of(n * ROW_BLOCK, ROW_BLOCK), ROW_BLOCK), n * ROW_BLOCK)
            return carry

        lax.fori_loop(0, rows // ROW_BLOCK, one, 0)

    def q_move(c, out):
        inner, outer = q_s.at[here(lax.rem(c, PAIR) * q_rows, q_rows)], q_hbm.at[here(c * q_rows, q_rows)]
        sem = q_sem.at[lax.rem(c, PAIR)]
        return pltpu.make_async_copy(inner, outer, sem) if out else pltpu.make_async_copy(outer, inner, sem)

    def raw_copy(layer, k):
        return pltpu.make_async_copy((kc, vc)[k].at[layer], q_s, raw_sem)

    def table_copies(c):
        return [pltpu.make_async_copy(tab.at[here(position(c, i), rows)], t_s.at[k, pl.ds(i * rows, rows)], t_sem) for i in range(GROUP) for k, tab in enumerate((cos, sin))]

    def pushes(layer, some=slice(None)):
        pairs = ((wk, qkv_peer.at[layer, :, pl.ds(PAIR * hd, hd)]), (wv, qkv_peer.at[layer, :, pl.ds(3 * hd, hd)]), (wq, qkv_peer.at[layer, :, pl.ds(0, PAIR * hd)]),
                 (wo, wo_peer.at[layer]), (up, up_peer.at[layer]), (down, down_peer.at[layer]))
        return [remote(src.at[layer], dst, p_send.at[layer, k], p_recv.at[layer, k], place.peer) for k, (src, dst) in list(enumerate(pairs))[some]]

    def norm_into(layer, which, c, slot):
        gain, shift = one_row(norms.at[layer], which), one_row(norms.at[layer], which + 1)

        def body(at, _):
            xo_s[slot, at, :] = normalized(mid_s[c, at, :].astype(F32), gain, shift)

        row_blocks(body)

    def slot_of(layer, ahead):
        return lambda c: lax.rem(c + (SLOTS - layer + ahead), SLOTS)

    spot = [slot_of(layer, 0) for layer in range(layers)]
    spare = [(SLOTS - 1 - layer) % SLOTS for layer in range(layers)]
    gather1 = [Gather(place, xo_s, spot[layer], a1_send, a1_recv, rows) for layer in range(layers)]
    h_loads = [pltpu.make_async_copy(tokens.at[pl.ds(c * rows, rows)], mid_s.at[c], h_sem.at[c]) for c in range(chunks)]
    for copy in h_loads:
        copy.start()
    raw_copy(0, 0).start()
    place.barrier((place.x, place.y, place.peer))

    def lead(layer, c):
        if layer == 0:
            h_loads[c].wait()
            norm_into(0, 0, c, spot[0](c))
        gather1[layer].start(c)

    lead(0, 0)
    lead(0, 1)
    b_copies = [remote(src, dst, b_send.at[k], b_recv.at[k], place.peer) for k, (src, dst) in enumerate(((bq_push, bq_s), (bk_push, bk_s), (bv_push, bv_s), (bu_push, bu_s)))]
    for copy in b_copies + pushes(0):
        copy.start()
    for copy in b_copies:
        copy.wait_recv()

    def project_phase(layer):
        gather = gather1[layer]
        base_new = [region(g, True) for g in range(PAIR)]
        old_push = remote(big_s.at[pl.ds(0, window)], big_s.at[pl.ds(window, window)], old_send, old_recv, place.peer)
        n_passes = chunks + 1

        def wa_fetch(n):
            t = lax.rem(n, GROUP)
            slot = lax.rem(n, PAIR)
            dst = pl.ds(pl.multiple_of(slot * model, tile), model)
            sem = wa_sem.at[slot]
            sources = (((wk.at[layer], 0, hd), (wv.at[layer], hd, hd)), ((qkv_peer.at[layer, :, pl.ds(PAIR * hd, PAIR * hd)], 0, PAIR * hd),),
                       ((wq.at[layer], 0, PAIR * hd),), ((qkv_peer.at[layer, :, pl.ds(0, PAIR * hd)], 0, PAIR * hd),))
            for k, made in enumerate(sources):
                @pl.when(jnp.logical_and(t == k, n < n_passes * GROUP))
                def _():
                    for src, at, width in made:
                        pltpu.make_async_copy(src, wo_s.at[dst, pl.ds(at, width)], sem).start()

        def wa_landed(n):
            slot = lax.rem(n, PAIR)
            at = pl.ds(pl.multiple_of(slot * model, tile), model)
            whole(wo_s.at[at], wa_sem.at[slot])
            wa_fetch(n + 1)
            return at

        def kv_copies(c, i):
            at = position(c, i)
            return [remote(big_s.at[here(base_new[g] + at, rows)], big_s.at[here(base_new[1 - g] + at, rows)], kv_send.at[c], kv_recv.at[c], place.peer) for g in range(PAIR)]

        wa_fetch(jnp.int32(0))
        for copy in table_copies(0):
            copy.start()

        def put_old(k):
            def put(n, turned):
                big_s[pl.ds(pl.multiple_of(n * ROLL_ROWS, ROLL_ROWS), ROLL_ROWS), k * hd:(k + 1) * hd] = turned[0]

            return put

        raw = [lambda: q_s[...]]
        raw_copy(layer, 0).wait()
        rotate(raw, put_old(0), window, first_slot, 0, roll_tiles)
        raw_copy(layer, 1).start()
        gather.forward(0)
        lead(layer, 2)
        raw_copy(layer, 1).wait()
        rotate(raw, put_old(1), window, first_slot, 0, roll_tiles)
        if layer > 0:
            pl.semaphore_wait(ready, 1)
        old_push.start()
        gather.forward(1)
        for g, (for_q, for_k, for_v) in enumerate(((bq, bk, bv), (bq_s, bk_s, bv_s))):
            ba_s[PAIR * g] = one_row(for_q, layer)
            ba_s[PAIR * g + 1, :, :hd] = one_row(for_k, layer)
            ba_s[PAIR * g + 1, :, hd:] = one_row(for_v, layer)
        for copy in pushes(layer, slice(0, 3)):
            copy.wait_recv()

        def state_copy(b):
            return pltpu.make_async_copy(st_s.at[lax.rem(b, PAIR)], state.at[b], st_sem.at[lax.rem(b, PAIR)])

        def attend_old(c, i):
            b = c * GROUP + i
            w = lax.rem(b, PAIR)
            j0 = position(c, i)
            diag = lax.div(j0, tile)
            i_next = jnp.minimum(i + 1, GROUP - 1)
            diag_next = lax.div(position(c, i_next), tile)

            @pl.when(b >= PAIR)
            def _():
                state_copy(b - PAIR).wait()

            reset_state(st_s, w)

            def step(t, by_row):
                at = t * tile
                last = t + 1 == tiles
                at_next = jnp.where(last, diag_next, t + 1) * tile
                n_i = jnp.where(last, i_next, i)
                age = lax.broadcasted_iota(jnp.int32, (1, tile), 1) + at
                if by_row:
                    row = lax.rem(lax.broadcasted_iota(jnp.int32, (tall, 1), 0), rows) + j0
                    mask = age > jnp.maximum(row, floor)
                else:
                    mask = age > floor
                flash_step(st_s, w, s_s, scale, mask, lambda g: tile_of(g, False, at, 1), lambda g: scores(c, n_i, g, False, at_next))

            step(diag, True)

            def younger(t, carry):
                @pl.when(t > diag)
                def _():
                    step(t, False)

                return carry

            lax.fori_loop(1, tiles, younger, 0)
            state_copy(b).start()

        def one_pass(p, carry):
            c = jnp.minimum(p, last_chunk)
            upper = p != n_passes - 1
            lower = p != n_passes - PAIR

            @pl.when(upper)
            def _():
                whole(t_s, t_sem)

            @pl.when(lower)
            def _():
                gather.finish(c)

            slot = spot[layer](c)

            def rope(u, i):
                turned = jnp.concatenate([-u[:, hd // 2:], u[:, :hd // 2]], axis=1)
                return (u * t_s[0, i * rows:(i + 1) * rows, :] + turned * t_s[1, i * rows:(i + 1) * rows, :]).astype(BF16)

            parts = ((upper, 0, GROUP - 1), (lower, GROUP - 1, 1))

            def keys_values(g, inner):
                at = wa_landed(p * GROUP + g)
                for wanted, i0, count in parts:
                    @pl.when(wanted)
                    def _():
                        r0, n = i0 * rows, count * rows
                        u = jnp.dot(xo_s[slot, r0:r0 + n, :], wo_s[at, :], preferred_element_type=F32) + ba_s[PAIR * g + 1]
                        for i in range(count):
                            to = here(region(g, True) + position(c, i0 + i), rows)
                            part = u[i * rows:(i + 1) * rows]
                            big_s[to, :hd] = rope(part[:, :hd], i0 + i)
                            big_s[to, hd:] = part[:, hd:].astype(BF16)
                return inner

            lax.fori_loop(0, PAIR, keys_values, 0)
            for i in range(GROUP):
                @pl.when(upper if i < GROUP - 1 else lower)
                def _():
                    for copy in kv_copies(c, i):
                        copy.start()

            @pl.when(jnp.logical_and(upper, c >= PAIR))
            def _():
                q_move(c - PAIR, True).wait()

            def for_queries(g, inner):
                at = wa_landed(p * GROUP + PAIR + g)
                for wanted, i0, count in parts:
                    @pl.when(wanted)
                    def _():
                        r0, n = i0 * rows, count * rows
                        u = jnp.dot(xo_s[slot, r0:r0 + n, :], wo_s[at, :], preferred_element_type=F32) + ba_s[PAIR * g]
                        for h in range(PAIR):
                            for i in range(count):
                                part = u[i * rows:(i + 1) * rows, h * hd:(h + 1) * hd]
                                q_s[here(q_row(c, g, i0 + i) + h * rows, rows), :] = rope(part, i0 + i)
                return inner

            lax.fori_loop(0, PAIR, for_queries, 0)

            @pl.when(lower)
            def _():
                q_move(c, True).start()

            @pl.when(c < last_chunk)
            def _():
                for copy in table_copies(c + 1):
                    copy.start()

            @pl.when(p == 0)
            def _():
                old_push.wait_recv()

            @pl.when(jnp.logical_or(p == 0, p == 2))
            def _():
                early = lax.div(p, 2)
                for g in range(PAIR):
                    s_s[g] = scores(early, 0, g, False, lax.div(position(early, 0), tile) * tile)

                def one(i, inner):
                    @pl.when(jnp.logical_and(p == 2, i == 3))
                    def _():
                        gather.forward(3)

                    attend_old(early, i)
                    return inner

                lax.fori_loop(0, GROUP, one, 0)

            @pl.when(p == 0)
            def _():
                gather.forward(2)
                lead(layer, 3)

            @pl.when(p == 2)
            def _():
                q_move(2, True).wait()
                q_move(0, False).start()

            return carry

        lax.fori_loop(0, n_passes, one_pass, 0)
        q_move(last_chunk, True).wait()
        q_move(1, False).start()
        whole_chunk = big_s.at[pl.ds(0, PAIR * GROUP * rows)]
        kv_all = [remote(whole_chunk, whole_chunk, kv_send.at[c], kv_recv.at[c], place.peer) for c in range(chunks)]
        for copy in kv_all:
            copy.wait_recv()
        for copy in kv_all + [old_push]:
            copy.wait_send()
        for b in range(GROUP * EARLY - PAIR, GROUP * EARLY):
            state_copy(jnp.int32(b)).wait()
        for c in range(chunks):
            gather.drain(c)

    def block_phase(layer):
        onward = layer + 1 < layers
        gather = Gather(place, xo_s, spot[layer], a2_send, a2_recv, rows)
        first = Scatter(place, xo_s, slot_of(layer, 1), land_s, r1_send, r1_recv, rows)
        second = Scatter(place, xo_s, spot[layer], land_s, r2_send, r2_recv, rows)
        pushes(layer, slice(3, 4))[0].wait_recv()
        n_out = model // WIDE
        for n in range(n_out):
            for k, src in enumerate((wo, wo_peer)):
                pltpu.make_async_copy(src.at[layer, :, pl.ds(n * WIDE, WIDE)], wo_s.at[pl.ds(n * deep + k * PAIR * hd, PAIR * hd)], wo_sem).start()
        if onward:
            for copy in pushes(layer + 1):
                copy.start()

        def pick(k):
            return jnp.where(k == 0, 3, jnp.where(k == 3, 0, k))

        def state_copy(b):
            slot = lax.rem(b, PAIR)
            return pltpu.make_async_copy(state.at[lax.div(b, GROUP) * GROUP + pick(lax.rem(b, GROUP))], st_s.at[slot], st_sem.at[slot])

        for b in range(PAIR):
            state_copy(jnp.int32(b)).start()

        def tile_at(diag, n):
            is_new = jnp.logical_or(n == 0, jnp.logical_and(n >= 2, n - 2 < diag))
            t = jnp.where(n < 2, diag, jnp.where(is_new, n - 2, n - 1))
            return is_new, t * tile

        q_move(jnp.int32(0), False).wait()
        for g in range(PAIR):
            s_s[g] = scores(jnp.int32(0), 3, g, True, lax.div(position(0, 3), tile) * tile)

        def attend(c, k):
            i = pick(k)
            b = c * GROUP + k
            w = lax.rem(b, PAIR)
            late = c >= EARLY
            j0 = position(c, i)
            diag = lax.div(j0, tile)
            count = jnp.where(late, tiles + 1, diag + 2)
            end = k == 3
            c_next = jnp.minimum(jnp.where(end, c + 1, c), last_chunk)
            i_next = pick(jnp.where(end, 0, k + 1))
            next_at = lax.div(position(c_next, i_next), tile) * tile

            @pl.when(late)
            def _():
                reset_state(st_s, w)

            @pl.when(jnp.logical_not(late))
            def _():
                state_copy(b).wait()

            def step(n):
                is_new, at = tile_at(diag, n)
                following = jnp.where(jnp.logical_and(n == 0, jnp.logical_not(late)), 2, n + 1)
                last = following == count
                new_next, at_next = tile_at(diag, following)
                new_next = jnp.logical_or(last, new_next)
                at_next = jnp.where(last, next_at, at_next)
                nc = jnp.where(last, c_next, c)
                ni = jnp.where(last, i_next, i)
                col = lax.broadcasted_iota(jnp.int32, (1, tile), 1) + at
                row = lax.rem(lax.broadcasted_iota(jnp.int32, (tall, 1), 0), rows) + j0
                if not isinstance(n, int):
                    mask = col > jnp.where(is_new, -1, floor)
                elif n == 0:
                    mask = col <= row
                else:
                    mask = col > jnp.maximum(row, floor)
                flash_step(st_s, w, s_s, scale, mask, lambda g: tile_of(g, is_new, at, 1), lambda g: scores(nc, ni, g, new_next, at_next))

            step(0)

            @pl.when(late)
            def _():
                step(1)

            def further(n, carry):
                @pl.when(n < count)
                def _():
                    step(n)

                return carry

            lax.fori_loop(2, tiles + 1, further, 0)
            slot = first.slot(c)
            for g in range(PAIR):
                total = jnp.sum(st_s[w, g, :, LANES:PAIR * LANES], axis=1, keepdims=True)
                out = (st_s[w, g, :, PAIR * LANES:] / total).astype(BF16)
                for h in range(PAIR):
                    n = PAIR * g + h
                    xo_s[slot, :rows, n * hd:(n + 1) * hd] = out[h * rows:(h + 1) * rows]

            @pl.when(b + PAIR < GROUP * EARLY)
            def _():
                state_copy(b + PAIR).start()

            @pl.when(b == 0)
            def _():
                whole(wo_s, wo_sem)

            to = here(i * rows, rows)

            def summed(n):
                return jnp.dot(xo_s[slot, :rows, :deep], wo_s[n * deep:(n + 1) * deep, :], preferred_element_type=F32).astype(BF16)

            held = deep // WIDE
            for n in range(held, n_out):
                xo_s[slot, to, n * WIDE:(n + 1) * WIDE] = summed(n)
            for n, part in enumerate([summed(n) for n in range(held)]):
                xo_s[slot, to, n * WIDE:(n + 1) * WIDE] = part

            @pl.when(i == 3)
            def _():
                first.copy(c, 0).start()
                first.copy(c, 1).start()

            for kind in (2, 3):
                @pl.when(i == kind - 1)
                def _():
                    first.copy(c, kind).start()

        bias_o, bias_d = one_row(b_o, layer), one_row(b_down, layer)

        def open_mlp(c):
            first.finish(c)

            def body(at, n):
                mid_s[c, at, :] = (mid_s[c, at, :].astype(F32) + first.total(c, n) + bias_o).astype(BF16)

            row_blocks(body)
            norm_into(layer, 2, c, spot[layer](c))
            gather.start(c)

        def attend_chunk(c, carry):
            def one(k, inner):
                @pl.when(jnp.logical_and(k == 3, c + 1 < chunks))
                def _():
                    q_move(c + 1, False).wait()

                attend(c, k)

                @pl.when(jnp.logical_and(k == 1, c >= 1))
                def _():
                    first.relay(c - 1, c - 2)

                return inner

            lax.fori_loop(0, GROUP, one, 0)

            @pl.when(c + PAIR < chunks)
            def _():
                q_move(c + PAIR, False).start()

            @pl.when(c >= 2)
            def _():
                open_mlp(c - 2)

            return carry

        lax.fori_loop(0, chunks, attend_chunk, 0)
        if onward:
            raw_copy(layer + 1, 0).start()
        for copy in pushes(layer, slice(4, None)):
            copy.wait_recv()
        n_up = PAIR * ffn // WIDE
        n_tiles = n_up + n_out
        sub = WIDE // PAIR
        n_sub = ffn // sub
        act = xo_s.at[spare[layer]]

        def slot_at(c, k):
            slot = lax.rem(c * n_tiles + k, WEIGHT_SLOTS)
            return slot, pl.multiple_of(slot * model, WIDE)

        def fetch(c, k):
            over = k >= n_tiles
            k = jnp.where(over, k - n_tiles, k)
            c = jnp.where(over, c + 1, c)
            slot, base = slot_at(c, k)

            @pl.when(c < chunks)
            def _():
                for part in range(PAIR):
                    n = PAIR * k + part
                    for side, src in enumerate((up, up_peer)):
                        @pl.when(jnp.logical_and(n >= side * n_sub, n < (side + 1) * n_sub))
                        def _():
                            at = pl.multiple_of((n - side * n_sub) * sub, sub)
                            pltpu.make_async_copy(src.at[layer, :, pl.ds(at, sub)], big_s.at[pl.ds(base, model), pl.ds(part * sub, sub)], wm_sem.at[slot]).start()

                @pl.when(k >= n_up)
                def _():
                    at = pl.multiple_of((k - n_up) * WIDE, WIDE)
                    for side, src in enumerate((down, down_peer)):
                        dst = big_s.at[pl.ds(pl.multiple_of(base + side * ffn, sub), ffn)]
                        pltpu.make_async_copy(src.at[layer, :, pl.ds(at, WIDE)], dst, wm_sem.at[slot]).start()

        def landed(c, k):
            slot, base = slot_at(c, k)
            whole(big_s.at[pl.ds(base, model)], wm_sem.at[slot])
            fetch(c, k + WEIGHT_SLOTS - 1)
            return pl.ds(base, model)

        for k in range(WEIGHT_SLOTS - 1):
            fetch(jnp.int32(0), jnp.int32(k))
        stage = WEIGHT_SLOTS * model

        def stage_at(n):
            slot = lax.rem(n, ROLL_SLOTS)
            return slot, pl.ds(pl.multiple_of(stage + slot * ROLL_ROWS, ROLL_ROWS), ROLL_ROWS)

        def staged(n):
            slot, at = stage_at(n)
            whole(big_s.at[at], f_sem.at[slot])

        def put_new(n, turned):
            slot, at = stage_at(n)

            @pl.when(n >= ROLL_SLOTS)
            def _():
                staged(n)

            for k in range(PAIR):
                cols = slice(k * hd, (k + 1) * hd)
                big_s[at, cols] = turned[k]
                dst = pl.ds(pl.multiple_of((layer * PAIR + k) * window + n * ROLL_ROWS, ROLL_ROWS), ROLL_ROWS)
                pltpu.make_async_copy(big_s.at[at, cols], kv_rolled.at[dst], f_sem.at[slot]).start()

        fresh = [lambda k=k: big_s[3 * window:, k * hd:(k + 1) * hd] for k in range(PAIR)]
        rotate(fresh, put_new, window, window - first_slot, 0, roll_tiles // PAIR)
        gather.forward(0)
        rotate(fresh, put_new, window, window - first_slot, roll_tiles // PAIR, roll_tiles)
        for n in range(PAIR * n_sub):
            src = bu if n < n_sub else bu_s
            at = n % n_sub * sub
            bm_s[n // PAIR, :, n % PAIR * sub:(n % PAIR + 1) * sub] = one_row(src, layer)[:, at:at + sub]
        first.relay(last_chunk, last_chunk - 1)
        open_mlp(2)
        gather.forward(1)
        open_mlp(3)
        first.drain(last_chunk)
        for n in range(ROLL_SLOTS):
            staged(n)

        def mlp_chunk(c, carry):
            gather.finish(c)
            slot = spot[layer](c)

            def up_step(k, inner):
                at = landed(c, k)
                for top in range(PAIR):
                    r0 = top * tall
                    lifted = jnp.dot(xo_s[slot, r0:r0 + tall, :], big_s[at, :], preferred_element_type=F32) + bm_s[k]
                    act[r0:r0 + tall, pl.ds(pl.multiple_of(k * WIDE, WIDE), WIDE)] = gelu_tanh(lifted).astype(BF16)
                return inner

            lax.fori_loop(0, n_up, up_step, 0)

            @pl.when(c + 2 < chunks)
            def _():
                gather.forward(c + 2)

            gather.drain(c)

            @pl.when(c >= 2)
            def _():
                second.relay(c - 2, c - 3)

            def down_step(k, inner):
                at = landed(c, k)
                xo_s[slot, :, pl.ds(pl.multiple_of((k - n_up) * WIDE, WIDE), WIDE)] = jnp.dot(act[...], big_s[at, :], preferred_element_type=F32).astype(BF16)
                return inner

            lax.fori_loop(n_up, n_tiles, down_step, 0)
            second.start(c)
            return carry

        lax.fori_loop(0, chunks, mlp_chunk, 0)
        if onward:
            pl.semaphore_signal(ready, inc=1, device_id={'tp': place.peer}, device_id_type=MESH)

        def o_copy(c):
            return pltpu.make_async_copy(mid_s.at[c], h_out.at[here(c * rows, rows)], h_sem.at[c])

        second.relay(2, 1)
        second.relay(3, 2)

        def close(c, carry):
            second.finish(c)

            def body(at, n):
                mid_s[c, at, :] = (mid_s[c, at, :].astype(F32) + second.total(c, n) + bias_d).astype(BF16)

            row_blocks(body)
            if onward:
                norm_into(layer + 1, 0, c, spot[layer + 1](c))

                @pl.when(c < 2)
                def _():
                    lead(layer + 1, c)
            else:
                o_copy(c).start()
            return carry

        lax.fori_loop(0, chunks, close, 0)
        second.drain(last_chunk)
        if not onward:
            for c in range(chunks):
                o_copy(c).wait()

    for layer in range(layers):
        project_phase(layer)
        block_phase(layer)
    for copy in b_copies:
        copy.wait_send()
    for layer in range(layers):
        for copy in pushes(layer):
            copy.wait_send()


def run_step(chunks, scal, tokens, norms, cos, sin, weights, biases, caches, w_o, w_up, w_down, b_o, b_down):
    model = tokens.shape[1]
    rows = tokens.shape[0] // chunks
    layers, window, hd = caches[0].shape
    ffn = w_up.shape[2]
    dims = (layers, chunks, rows, model, hd, window, ffn)
    state = (GROUP * EARLY, PAIR, PAIR * rows, PAIR * LANES + hd)
    out = [tokens.shape, (layers * PAIR * window, hd), (chunks * PAIR * GROUP * PAIR * rows, hd), (layers, model, GROUP * hd), w_o.shape, w_up.shape, w_down.shape]
    out = [jax.ShapeDtypeStruct(o, BF16) for o in out]
    out.insert(3, jax.ShapeDtypeStruct(state, F32))
    few = [dma(*n) for n in ((chunks,), (), (), (PAIR,), (), (WEIGHT_SLOTS,), (PAIR,), (PAIR,), (ROLL_SLOTS,))]
    return pl.pallas_call(
        functools.partial(step_kernel, dims),
        out_shape=tuple(out),
        in_specs=[SMEM, ANY, VMEM] + [ANY] * 5 + [VMEM] * 4 + [ANY] * 9 + [VMEM] * 2,
        out_specs=(ANY,) * len(out),
        scratch_shapes=[
            vm(PAIR * PAIR * window, WIDE),
            vm(window, hd),
            vm(PAIR, GROUP * rows, hd, dtype=F32),
            vm(PAIR, PAIR * rows, KEY_TILE, dtype=F32),
            vm(PAIR * model, WIDE),
            vm(SLOTS, GROUP * rows, model),
            vm(chunks, 3 * rows, model),
            vm(chunks, rows, model),
            vm(PAIR, *state[1:], dtype=F32),
            vm(GROUP, 1, PAIR * hd, dtype=F32),
            vm(PAIR * ffn // WIDE, 1, WIDE, dtype=F32),
            *(vm(*b.shape) for b in biases),
            *(dma(chunks, GROUP) for _ in range(GROUP)),
            *(dma(chunks, 6) for _ in range(GROUP)),
            dma(),
            dma(),
            dma(chunks),
            dma(chunks),
            dma(layers, 6),
            dma(layers, 6),
            dma(GROUP),
            dma(GROUP),
            *few,
            pltpu.SemaphoreType.REGULAR,
        ],
        compiler_params=pltpu.CompilerParams(vmem_limit_bytes=VMEM_LIMIT, collective_id=0, has_side_effects=True),
        name="step",
    )(scal, tokens, norms, cos, sin, *weights, *biases, *biases, *caches, w_o, w_up, w_down, b_o, b_down)


def copy_kernel(scal, *refs):
    hidden, kv, h_out, k_out, v_out, p_out, h_s, kv_s, in_sem, out_sem = refs
    window = k_out.shape[1]
    cut = window // PAIR
    part = hidden.shape[0] // PAIR
    moves = [(hidden.at[pl.ds(n * part, part)], h_s.at[pl.ds(n * part, part)], h_out.at[pl.ds(n * part, part)]) for n in range(PAIR)]
    for layer in range(k_out.shape[0]):
        for k, out in enumerate((k_out, v_out)):
            for n in range(PAIR):
                at = pl.ds((layer * PAIR + k) * window + n * cut, cut)
                moves.append((kv.at[at], kv_s.at[at], out.at[layer, pl.ds(n * cut, cut)]))
    for n, (src, mid, _) in enumerate(moves):
        pltpu.make_async_copy(src, mid, in_sem.at[n]).start()
    start_pos = scal[0]
    ahead = lax.broadcasted_iota(jnp.int32, p_out.shape, 1) + (window - lax.rem(start_pos, window))
    p_out[...] = start_pos + jnp.where(ahead >= window, ahead - window, ahead)
    for n, (src, mid, dst) in enumerate(moves):
        pltpu.make_async_copy(src, mid, in_sem.at[n]).wait()
        pltpu.make_async_copy(mid, dst, out_sem.at[n]).start()
    for n, (_, mid, dst) in enumerate(moves):
        pltpu.make_async_copy(mid, dst, out_sem.at[n]).wait()


def run_copy(scal, hidden, kv, layers, window):
    hd = kv.shape[1]
    planes = jax.ShapeDtypeStruct((layers, window, hd), BF16)
    count = PAIR + PAIR * PAIR * layers
    return pl.pallas_call(
        copy_kernel,
        out_shape=(jax.ShapeDtypeStruct(hidden.shape, BF16), planes, planes, jax.ShapeDtypeStruct((1, window), jnp.int32)),
        in_specs=[SMEM, ANY, ANY],
        out_specs=(ANY, ANY, ANY, VMEM),
        scratch_shapes=[vm(*hidden.shape), vm(*kv.shape), dma(count), dma(count)],
        compiler_params=pltpu.CompilerParams(vmem_limit_bytes=VMEM_LIMIT),
        name="copy_out",
    )(scal, hidden, kv)


def solution(mesh):
    row_spec = P('dp', 'tp', None)
    cache_spec = P(None, 'dp', None, 'tp', None)
    col_spec = P(None, None, 'tp')
    bias_spec = P(None, 'tp')
    in_specs = (row_spec, P('dp'), P('dp', None, None), P('dp', None, None), cache_spec, cache_spec, P('dp', None), P(), col_spec, bias_spec, col_spec, bias_spec, col_spec, bias_spec, P(None, 'tp', None), P(), col_spec, bias_spec, P(None, 'tp', None), P())
    out_specs = (row_spec, cache_spec, cache_spec, P('dp', None))

    def device_step(tokens, start_pos, cos_tab, sin_tab, key_cache, value_cache, slot_pos, norm_params, w_q, b_q, w_k, b_k, w_v, b_v, w_o, b_o, w_up, b_up, w_down, b_down):
        layers, _, window, _, hd = key_cache.shape
        caches = tuple(cache.reshape(layers, window, hd) for cache in (key_cache, value_cache))
        made = run_step(CHUNKS, start_pos, tokens[0], norm_params, cos_tab[0], sin_tab[0], (w_q, w_k, w_v), (b_q, b_k, b_v, b_up), caches, w_o, w_up, w_down, b_o, b_down)
        hidden, key_out, value_out, pos_out = run_copy(start_pos, made[0], made[1], layers, window)
        return hidden[None], key_out.reshape(key_cache.shape), value_out.reshape(value_cache.shape), pos_out

    return jax.shard_map(device_step, mesh=mesh, in_specs=in_specs, out_specs=out_specs, check_vma=False)
```

time: 2370 us -> 1010 us (0.43)
  waiting for transfers between devices: 1120 us -> 0 us
  Pallas kernels: 0 us -> 1000 us
  matrix products: 851 us -> 0 us
  other arithmetic: 336 us -> 0 us
  local copies, waits for them, and re-layouts: 47.7 us -> 0 us
    pallas_call x0 -> x2, Pallas kernels: none -> 1000 us  [the longest x1 994 us: run_step(): pl.pallas_call(functools.partial(step_kernel, dims), out_shape=tuple(out)...]
    dot_general x20 -> x0, matrix products: 851 us -> none  [the longest x8 229 us: project(): jnp.einsum('bcm,mn->bcn', acts, weight, preferred_element_type=jnp.float32)]
    reduce_scatter x4 -> x0, waiting for transfers between devices: 619 us -> none  [device_step(): summed = lax.psum_scatter(part_sum, 'tp', scatter_dimension=1, tiled=True)]
    all_gather x4 -> x0, waiting for transfers between devices: 498 us -> none  [device_step(): gathered = lax.all_gather(normed, 'tp', axis=1, tiled=True)]
    reduce_sum x10 -> x0, other arithmetic: 207 us -> none  [the longest x2 184 us: local_attention(): total = jnp.sum(exp_old, axis=-1) + jnp.sum(exp_new, axis=-1)]
    convert_element_type x14 -> x0, other arithmetic: 56.9 us -> none  [the longest x3 32 us: apply_rotary(): return (values * cos_b + turned * sin_b).astype(jnp.bfloat16)]
    unnamed x80 -> x0, local copies, waits for them, and re-layouts: 47.7 us -> none
  transfers between devices with their start and end apart: 8 -> 0, of which waited for: 8 -> 0; matrix products, arithmetic and copies ran while one was open for 4% -> 0% of each run, Pallas kernels for 0% -> 0%
where the time goes in v1:
time: 1010 us
  Pallas kernels  1000 us (99%)
    pallas_call x1, Pallas kernels, run_step(): pl.pallas_call(functools.partial(step_kernel, dims), out_shape=tuple(out)...  994 us

profile of v1, /device:TPU:0, one launch (start us, length us, event | category | flops | bytes accessed | tf_op | source)
XLA Modules:
  0.0 1005.7 jit_solution(3052928703815645011)
XLA Ops:
  1.3 994.4 %step.1 = (bf16[512,3584]{1,0:T(8,128)(2,1)}, bf16[16384,256]{1,0:T(8,128)(2,1)}, bf16[8192,256]{1,0:T(8,128)(2,1)}, f32[8,2,256,512]{3,2,1,0:T(8,128)}, bf16[2,...) custom-call(s32[1]{0:T(128)S(6)} %copy.25.scal, ...), custom_call_target="tpu_custom_call" | custom-call | tf_op jit(solution)/shard_map/step/pallas_call | solution.py:854
  995.7 9.8 copy_out.1

commit v2 on v1

--- a/solution.py
+++ b/solution.py
@@ -131,26 +131,30 @@
 
     def copy(self, c, kind):
         r, h = self.rows, self.rows // 2
-        src, dst, size, other = ((0, r, r, self.place.x), (0, 2 * r, r, self.place.y), (r, 3 * r, h, self.place.y), (2 * r + h, 3 * r + h, h, self.place.x))[kind]
+        x, y = self.place.x, self.place.y
+        src, dst, other = ((0, r, x), (h, 2 * r + h, y), (h, r + h, x), (0, 2 * r, y), (r, 3 * r, y), (2 * r + h, 3 * r + h, x))[kind]
         slot = self.slot(c)
-        return remote(self.x_s.at[slot, pl.ds(src, size)], self.x_s.at[slot, pl.ds(dst, size)], self.send.at[c, kind], self.recv.at[c, kind], other)
+        return remote(self.x_s.at[slot, pl.ds(src, h)], self.x_s.at[slot, pl.ds(dst, h)], self.send.at[c, kind], self.recv.at[c, kind], other)
 
     def start(self, c):
-        self.copy(c, 0).start()
-        self.copy(c, 1).start()
+        for kind in range(4):
+            self.copy(c, kind).start()
 
     def forward(self, c):
-        self.copy(c, 0).wait_recv()
-        self.copy(c, 2).start()
-        self.copy(c, 1).wait_recv()
-        self.copy(c, 3).start()
+        for kind in range(2):
+            self.copy(c, kind).wait_recv()
+            self.copy(c, kind + 4).start()
+
+    def near(self, c):
+        for kind in (2, 3):
+            self.copy(c, kind).wait_recv()
 
     def finish(self, c):
-        self.copy(c, 2).wait_recv()
-        self.copy(c, 3).wait_recv()
+        for kind in (4, 5):
+            self.copy(c, kind).wait_recv()
 
     def drain(self, c):
-        for kind in range(GROUP):
+        for kind in range(6):
             self.copy(c, kind).wait_send()
 
 
@@ -183,9 +187,10 @@
 
             lax.fori_loop(0, h // ROW_BLOCK, block, 0)
 
-        @pl.when(settled >= 0)
-        def _():
-            self.drain(settled)
+        if settled is not None:
+            @pl.when(settled >= 0)
+            def _():
+                self.drain(settled)
 
         self.copy(c, 5).start()
         self.copy(c, 4).start()
@@ -300,9 +305,17 @@
     for copy in b_copies:
         copy.wait_recv()
 
+    def pick(k):
+        return jnp.where(k == 0, 3, jnp.where(k == 3, 0, k))
+
+    def state_move(b, out):
+        slot = lax.rem(b, PAIR)
+        if out:
+            return pltpu.make_async_copy(st_s.at[slot], state.at[b], st_sem.at[slot])
+        return pltpu.make_async_copy(state.at[lax.div(b, GROUP) * GROUP + pick(lax.rem(b, GROUP))], st_s.at[slot], st_sem.at[slot])
+
     def project_phase(layer):
         gather = gather1[layer]
-        base_new = [region(g, True) for g in range(PAIR)]
         old_push = remote(big_s.at[pl.ds(0, window)], big_s.at[pl.ds(window, window)], old_send, old_recv, place.peer)
         n_passes = chunks + 1
 
@@ -323,12 +336,11 @@
             slot = lax.rem(n, PAIR)
             at = pl.ds(pl.multiple_of(slot * model, tile), model)
             whole(wo_s.at[at], wa_sem.at[slot])
-            wa_fetch(n + 1)
             return at
 
-        def kv_copies(c, i):
+        def kv_copy(c, i, g):
             at = position(c, i)
-            return [remote(big_s.at[here(base_new[g] + at, rows)], big_s.at[here(base_new[1 - g] + at, rows)], kv_send.at[c], kv_recv.at[c], place.peer) for g in range(PAIR)]
+            return remote(big_s.at[here(region(g, True) + at, rows)], big_s.at[here(region(1 - g, True) + at, rows)], kv_send.at[c], kv_recv.at[c], place.peer)
 
         wa_fetch(jnp.int32(0))
         for copy in table_copies(0):
@@ -358,9 +370,7 @@
             ba_s[PAIR * g + 1, :, hd:] = one_row(for_v, layer)
         for copy in pushes(layer, slice(0, 3)):
             copy.wait_recv()
-
-        def state_copy(b):
-            return pltpu.make_async_copy(st_s.at[lax.rem(b, PAIR)], state.at[b], st_sem.at[lax.rem(b, PAIR)])
+        wa_fetch(jnp.int32(1))
 
         def attend_old(c, i):
             b = c * GROUP + i
@@ -372,7 +382,7 @@
 
             @pl.when(b >= PAIR)
             def _():
-                state_copy(b - PAIR).wait()
+                state_move(b - PAIR, True).wait()
 
             reset_state(st_s, w)
 
@@ -399,7 +409,7 @@
                 return carry
 
             lax.fori_loop(1, tiles, younger, 0)
-            state_copy(b).start()
+            state_move(b, True).start()
 
         def one_pass(p, carry):
             c = jnp.minimum(p, last_chunk)
@@ -409,6 +419,7 @@
             @pl.when(upper)
             def _():
                 whole(t_s, t_sem)
+                gather.near(c)
 
             @pl.when(lower)
             def _():
@@ -434,14 +445,12 @@
                             part = u[i * rows:(i + 1) * rows]
                             big_s[to, :hd] = rope(part[:, :hd], i0 + i)
                             big_s[to, hd:] = part[:, hd:].astype(BF16)
+                        for i in range(i0, i0 + count):
+                            kv_copy(c, i, g).start()
+                wa_fetch(p * GROUP + g + PAIR)
                 return inner
 
             lax.fori_loop(0, PAIR, keys_values, 0)
-            for i in range(GROUP):
-                @pl.when(upper if i < GROUP - 1 else lower)
-                def _():
-                    for copy in kv_copies(c, i):
-                        copy.start()
 
             @pl.when(jnp.logical_and(upper, c >= PAIR))
             def _():
@@ -458,6 +467,7 @@
                             for i in range(count):
                                 part = u[i * rows:(i + 1) * rows, h * hd:(h + 1) * hd]
                                 q_s[here(q_row(c, g, i0 + i) + h * rows, rows), :] = rope(part, i0 + i)
+                wa_fetch(p * GROUP + g + PAIR + PAIR)
                 return inner
 
             lax.fori_loop(0, PAIR, for_queries, 0)
@@ -481,11 +491,11 @@
                 for g in range(PAIR):
                     s_s[g] = scores(early, 0, g, False, lax.div(position(early, 0), tile) * tile)
 
+                @pl.when(p == 2)
+                def _():
+                    gather.forward(3)
+
                 def one(i, inner):
-                    @pl.when(jnp.logical_and(p == 2, i == 3))
-                    def _():
-                        gather.forward(3)
-
                     attend_old(early, i)
                     return inner
 
@@ -500,6 +510,9 @@
             def _():
                 q_move(2, True).wait()
                 q_move(0, False).start()
+                for b in range(PAIR):
+                    state_move(jnp.int32(GROUP * EARLY - PAIR + b), True).wait()
+                    state_move(jnp.int32(b), False).start()
 
             return carry
 
@@ -512,8 +525,6 @@
             copy.wait_recv()
         for copy in kv_all + [old_push]:
             copy.wait_send()
-        for b in range(GROUP * EARLY - PAIR, GROUP * EARLY):
-            state_copy(jnp.int32(b)).wait()
         for c in range(chunks):
             gather.drain(c)
 
@@ -531,16 +542,6 @@
             for copy in pushes(layer + 1):
                 copy.start()
 
-        def pick(k):
-            return jnp.where(k == 0, 3, jnp.where(k == 3, 0, k))
-
-        def state_copy(b):
-            slot = lax.rem(b, PAIR)
-            return pltpu.make_async_copy(state.at[lax.div(b, GROUP) * GROUP + pick(lax.rem(b, GROUP))], st_s.at[slot], st_sem.at[slot])
-
-        for b in range(PAIR):
-            state_copy(jnp.int32(b)).start()
-
         def tile_at(diag, n):
             is_new = jnp.logical_or(n == 0, jnp.logical_and(n >= 2, n - 2 < diag))
             t = jnp.where(n < 2, diag, jnp.where(is_new, n - 2, n - 1))
@@ -569,7 +570,7 @@
 
             @pl.when(jnp.logical_not(late))
             def _():
-                state_copy(b).wait()
+                state_move(b, False).wait()
 
             def step(n):
                 is_new, at = tile_at(diag, n)
@@ -614,7 +615,7 @@
 
             @pl.when(b + PAIR < GROUP * EARLY)
             def _():
-                state_copy(b + PAIR).start()
+                state_move(b + PAIR, False).start()
 
             @pl.when(b == 0)
             def _():
@@ -661,9 +662,9 @@
 
                 attend(c, k)
 
-                @pl.when(jnp.logical_and(k == 1, c >= 1))
+                @pl.when(jnp.where(c == 0, k == 3, jnp.logical_and(c >= 2, k == 0)))
                 def _():
-                    first.relay(c - 1, c - 2)
+                    first.relay(jnp.maximum(c - 1, 0), c - 2)
 
                 return inner
 
@@ -765,6 +766,7 @@
             staged(n)
 
         def mlp_chunk(c, carry):
+            gather.near(c)
             gather.finish(c)
             slot = spot[layer](c)
 
@@ -786,7 +788,7 @@
 
             @pl.when(c >= 2)
             def _():
-                second.relay(c - 2, c - 3)
+                second.relay(c - 2, c - 3 if onward else None)
 
             def down_step(k, inner):
                 at = landed(c, k)
@@ -804,8 +806,8 @@
         def o_copy(c):
             return pltpu.make_async_copy(mid_s.at[c], h_out.at[here(c * rows, rows)], h_sem.at[c])
 
-        second.relay(2, 1)
-        second.relay(3, 2)
+        second.relay(2, 1 if onward else None)
+        second.relay(3, 2 if onward else None)
 
         def close(c, carry):
             second.finish(c)
@@ -825,9 +827,11 @@
             return carry
 
         lax.fori_loop(0, chunks, close, 0)
-        second.drain(last_chunk)
-        if not onward:
+        if onward:
+            second.drain(last_chunk)
+        else:
             for c in range(chunks):
+                second.drain(c)
                 o_copy(c).wait()
 
     for layer in range(layers):
@@ -869,8 +873,7 @@
             vm(GROUP, 1, PAIR * hd, dtype=F32),
             vm(PAIR * ffn // WIDE, 1, WIDE, dtype=F32),
             *(vm(*b.shape) for b in biases),
-            *(dma(chunks, GROUP) for _ in range(GROUP)),
-            *(dma(chunks, 6) for _ in range(GROUP)),
+            *(dma(chunks, 6) for _ in range(8)),
             dma(),
             dma(),
             dma(chunks),
@@ -890,12 +893,12 @@
 def copy_kernel(scal, *refs):
     hidden, kv, h_out, k_out, v_out, p_out, h_s, kv_s, in_sem, out_sem = refs
     window = k_out.shape[1]
-    cut = window // PAIR
-    part = hidden.shape[0] // PAIR
-    moves = [(hidden.at[pl.ds(n * part, part)], h_s.at[pl.ds(n * part, part)], h_out.at[pl.ds(n * part, part)]) for n in range(PAIR)]
+    cut = window // GROUP
+    part = hidden.shape[0] // GROUP
+    moves = [(hidden.at[pl.ds(n * part, part)], h_s.at[pl.ds(n * part, part)], h_out.at[pl.ds(n * part, part)]) for n in range(GROUP)]
     for layer in range(k_out.shape[0]):
         for k, out in enumerate((k_out, v_out)):
-            for n in range(PAIR):
+            for n in range(GROUP):
                 at = pl.ds((layer * PAIR + k) * window + n * cut, cut)
                 moves.append((kv.at[at], kv_s.at[at], out.at[layer, pl.ds(n * cut, cut)]))
     for n, (src, mid, _) in enumerate(moves):
@@ -913,7 +916,7 @@
 def run_copy(scal, hidden, kv, layers, window):
     hd = kv.shape[1]
     planes = jax.ShapeDtypeStruct((layers, window, hd), BF16)
-    count = PAIR + PAIR * PAIR * layers
+    count = GROUP + PAIR * GROUP * layers
     return pl.pallas_call(
         copy_kernel,
         out_shape=(jax.ShapeDtypeStruct(hidden.shape, BF16), planes, planes, jax.ShapeDtypeStruct((1, window), jnp.int32)),

time: 1010 us -> 997 us (0.987)
  no operation moved by 1% of the time
where the time goes in v2:
time: 997 us; the launch traced here: 996 us
  Pallas kernels  995 us (100%)
    pallas_call x1, Pallas kernels, run_step(): pl.pallas_call(functools.partial(step_kernel, dims), out_shape=tuple(out)...  985 us

profile of v2, /device:TPU:0, one launch (start us, length us, event | category | flops | bytes accessed | tf_op | source)
XLA Modules:
  0.0 996.5 jit_solution(6623316892588740070)
XLA Ops:
  1.3 985.4 %step.1 = (bf16[512,3584]{1,0:T(8,128)(2,1)}, bf16[16384,256]{1,0:T(8,128)(2,1)}, bf16[8192,256]{1,0:T(8,128)(2,1)}, f32[8,2,256,512]{3,2,1,0:T(8,128)}, bf16[2,...) custom-call(s32[1]{0:T(128)S(6)} %copy.25.scal, ...), custom_call_target="tpu_custom_call" | custom-call | tf_op jit(solution)/shard_map/step/pallas_call | solution.py:858
  986.7 9.6 copy_out.1

commit v3 on v2

--- a/solution.py
+++ b/solution.py
@@ -77,9 +77,11 @@
         st_s[w, g, :, LANES:] = jnp.zeros((st_s.shape[2], st_s.shape[3] - LANES), F32)
 
 
-def flash_step(st_s, w, s_s, scale, mask, values, next_scores):
+def flash_step(st_s, w, s_s, scale, mask, values, next_scores, width=KEY_TILE):
     for g in range(PAIR):
-        s = jnp.where(mask, s_s[g] * scale, -jnp.inf)
+        s = s_s[g, :, :width] * scale
+        if mask is not None:
+            s = jnp.where(mask, s, -jnp.inf)
         s_next = next_scores(g)
         m_prev = st_s[w, g, :, 0:LANES]
         m_next = jnp.maximum(m_prev, jnp.max(s, axis=1, keepdims=True))
@@ -92,7 +94,7 @@
         st_s[w, g, :, 0:LANES] = m_next
         mixed = jnp.dot(e.astype(BF16), values(g), preferred_element_type=F32)
         st_s[w, g, :, 2 * LANES:] = st_s[w, g, :, 2 * LANES:] * jnp.concatenate([alpha] * (mixed.shape[1] // LANES), axis=1) + mixed
-        s_s[g] = s_next
+        s_s[g, :, :s_next.shape[1]] = s_next
 
 
 def score_tile(queries, keys):
@@ -248,12 +250,12 @@
     def scores(c, i, g, new, at):
         return score_tile(q_s[here(q_row(c, g, i), tall), :], tile_of(g, new, at, 0))
 
-    def row_blocks(body):
+    def row_blocks(body, first=0, last=rows):
         def one(n, carry):
             body(pl.ds(pl.multiple_of(n * ROW_BLOCK, ROW_BLOCK), ROW_BLOCK), n * ROW_BLOCK)
             return carry
 
-        lax.fori_loop(0, rows // ROW_BLOCK, one, 0)
+        lax.fori_loop(first // ROW_BLOCK, last // ROW_BLOCK, one, 0)
 
     def q_move(c, out):
         inner, outer = q_s.at[here(lax.rem(c, PAIR) * q_rows, q_rows)], q_hbm.at[here(c * q_rows, q_rows)]
@@ -271,13 +273,13 @@
                  (wo, wo_peer.at[layer]), (up, up_peer.at[layer]), (down, down_peer.at[layer]))
         return [remote(src.at[layer], dst, p_send.at[layer, k], p_recv.at[layer, k], place.peer) for k, (src, dst) in list(enumerate(pairs))[some]]
 
-    def norm_into(layer, which, c, slot):
+    def norm_into(layer, which, c, slot, *span):
         gain, shift = one_row(norms.at[layer], which), one_row(norms.at[layer], which + 1)
 
         def body(at, _):
             xo_s[slot, at, :] = normalized(mid_s[c, at, :].astype(F32), gain, shift)
 
-        row_blocks(body)
+        row_blocks(body, *span)
 
     def slot_of(layer, ahead):
         return lambda c: lax.rem(c + (SLOTS - layer + ahead), SLOTS)
@@ -294,6 +296,13 @@
     def lead(layer, c):
         if layer == 0:
             h_loads[c].wait()
+        if layer == 0 and c == 0:
+            for k in range(PAIR):
+                norm_into(0, 0, c, spot[0](c), k * rows // PAIR, (k + 1) * rows // PAIR)
+                for kind in (k, 3 - k):
+                    gather1[0].copy(c, kind).start()
+            return
+        if layer == 0:
             norm_into(0, 0, c, spot[0](c))
         gather1[layer].start(c)
 
@@ -317,7 +326,7 @@
     def project_phase(layer):
         gather = gather1[layer]
         old_push = remote(big_s.at[pl.ds(0, window)], big_s.at[pl.ds(window, window)], old_send, old_recv, place.peer)
-        n_passes = chunks + 1
+        n_passes = PAIR * chunks
 
         def wa_fetch(n):
             t = lax.rem(n, GROUP)
@@ -342,6 +351,8 @@
             at = position(c, i)
             return remote(big_s.at[here(region(g, True) + at, rows)], big_s.at[here(region(1 - g, True) + at, rows)], kv_send.at[c], kv_recv.at[c], place.peer)
 
+        whole_chunk = big_s.at[pl.ds(0, PAIR * GROUP * rows)]
+        kv_all = [remote(whole_chunk, whole_chunk, kv_send.at[c], kv_recv.at[c], place.peer) for c in range(chunks)]
         wa_fetch(jnp.int32(0))
         for copy in table_copies(0):
             copy.start()
@@ -377,7 +388,7 @@
             w = lax.rem(b, PAIR)
             j0 = position(c, i)
             diag = lax.div(j0, tile)
-            i_next = jnp.minimum(i + 1, GROUP - 1)
+            i_next = jnp.where(i < 2, i + 1, i)
             diag_next = lax.div(position(c, i_next), tile)
 
             @pl.when(b >= PAIR)
@@ -412,9 +423,9 @@
             state_move(b, True).start()
 
         def one_pass(p, carry):
-            c = jnp.minimum(p, last_chunk)
-            upper = p != n_passes - 1
-            lower = p != n_passes - PAIR
+            c = lax.div(p, PAIR)
+            lower = lax.rem(p, PAIR) == 1
+            upper = jnp.logical_not(lower)
 
             @pl.when(upper)
             def _():
@@ -476,7 +487,7 @@
             def _():
                 q_move(c, True).start()
 
-            @pl.when(c < last_chunk)
+            @pl.when(jnp.logical_and(lower, c < last_chunk))
             def _():
                 for copy in table_copies(c + 1):
                     copy.start()
@@ -485,44 +496,66 @@
             def _():
                 old_push.wait_recv()
 
-            @pl.when(jnp.logical_or(p == 0, p == 2))
-            def _():
-                early = lax.div(p, 2)
-                for g in range(PAIR):
-                    s_s[g] = scores(early, 0, g, False, lax.div(position(early, 0), tile) * tile)
-
-                @pl.when(p == 2)
-                def _():
-                    gather.forward(3)
-
-                def one(i, inner):
-                    attend_old(early, i)
-                    return inner
-
-                lax.fori_loop(0, GROUP, one, 0)
-
-            @pl.when(p == 0)
+            @pl.when(p == 2)
             def _():
                 gather.forward(2)
                 lead(layer, 3)
 
-            @pl.when(p == 2)
-            def _():
+            @pl.when(c < EARLY)
+            def _():
+                i0 = jnp.where(lower, 3, 0)
+                for g in range(PAIR):
+                    s_s[g] = scores(c, i0, g, False, lax.div(position(c, i0), tile) * tile)
+
+                def one(i, inner):
+                    @pl.when((i == 3) == lower)
+                    def _():
+                        attend_old(c, i)
+
+                    return inner
+
+                lax.fori_loop(0, GROUP, one, 0)
+
+            @pl.when(p == n_passes - 3)
+            def _():
+                gather.forward(3)
                 q_move(2, True).wait()
                 q_move(0, False).start()
                 for b in range(PAIR):
                     state_move(jnp.int32(GROUP * EARLY - PAIR + b), True).wait()
                     state_move(jnp.int32(b), False).start()
+                for copy in kv_all[:3]:
+                    copy.wait_recv()
+                q_move(0, False).wait()
+                state_move(jnp.int32(0), False).wait()
+                diag = lax.div(position(0, 3), tile)
+                width = 3 * rows
+
+                def keys(g, t, kv):
+                    return big_s[here(region(g, True) + t * tile, width), kv * hd:(kv + 1) * hd]
+
+                def ahead(t):
+                    return [score_tile(q_s[here(q_row(0, g, 3), tall), :], keys(g, t, 0)) for g in range(PAIR)]
+
+                for g, part in enumerate(ahead(0)):
+                    s_s[g, :, :width] = part
+
+                def earlier(t, inner):
+                    @pl.when(t < diag)
+                    def _():
+                        nxt = jnp.minimum(t + 1, tiles - 1)
+                        flash_step(st_s, 0, s_s, scale, None, lambda g: keys(g, t, 1), lambda g: score_tile(q_s[here(q_row(0, g, 3), tall), :], keys(g, nxt, 0)), width)
+
+                    return inner
+
+                lax.fori_loop(0, tiles - 1, earlier, 0)
 
             return carry
 
         lax.fori_loop(0, n_passes, one_pass, 0)
         q_move(last_chunk, True).wait()
         q_move(1, False).start()
-        whole_chunk = big_s.at[pl.ds(0, PAIR * GROUP * rows)]
-        kv_all = [remote(whole_chunk, whole_chunk, kv_send.at[c], kv_recv.at[c], place.peer) for c in range(chunks)]
-        for copy in kv_all:
-            copy.wait_recv()
+        kv_all[3].wait_recv()
         for copy in kv_all + [old_push]:
             copy.wait_send()
         for c in range(chunks):
@@ -547,7 +580,6 @@
             t = jnp.where(n < 2, diag, jnp.where(is_new, n - 2, n - 1))
             return is_new, t * tile
 
-        q_move(jnp.int32(0), False).wait()
         for g in range(PAIR):
             s_s[g] = scores(jnp.int32(0), 3, g, True, lax.div(position(0, 3), tile) * tile)
 
@@ -558,7 +590,7 @@
             late = c >= EARLY
             j0 = position(c, i)
             diag = lax.div(j0, tile)
-            count = jnp.where(late, tiles + 1, diag + 2)
+            count = jnp.where(b == 0, 2, jnp.where(late, tiles + 1, diag + 2))
             end = k == 3
             c_next = jnp.minimum(jnp.where(end, c + 1, c), last_chunk)
             i_next = pick(jnp.where(end, 0, k + 1))
@@ -568,7 +600,7 @@
             def _():
                 reset_state(st_s, w)
 
-            @pl.when(jnp.logical_not(late))
+            @pl.when(jnp.logical_and(jnp.logical_not(late), b > 0))
             def _():
                 state_move(b, False).wait()
 
@@ -596,6 +628,22 @@
             @pl.when(late)
             def _():
                 step(1)
+
+            def last_keys(u, carry):
+                @pl.when(jnp.logical_and(b == 0, u * GROUP < diag))
+                def _():
+                    def gathered(g, kv):
+                        cols = slice(kv * hd, (kv + 1) * hd)
+                        return jnp.concatenate([big_s[here(region(g, True) + (u * GROUP + n + 1) * tile - rows, rows), cols] for n in range(GROUP)], axis=0)
+
+                    for g in range(PAIR):
+                        s_s[g] = score_tile(q_s[here(q_row(c, g, i), tall), :], gathered(g, 0))
+                    seen = lax.broadcasted_iota(jnp.int32, (1, tile), 1) < (diag - u * GROUP) * rows
+                    flash_step(st_s, w, s_s, scale, seen, lambda g: gathered(g, 1), lambda g: scores(c_next, i_next, g, True, next_at))
+
+                return carry
+
+            lax.fori_loop(0, PAIR, last_keys, 0)
 
             def further(n, carry):
                 @pl.when(n < count)

time: 997 us -> 1000 us (level)
  no operation moved by 1% of the time
where the time goes in v3:
time: 1000 us
  Pallas kernels  1000 us (100%)
    pallas_call x1, Pallas kernels, run_step(): pl.pallas_call(functools.partial(step_kernel, dims), out_shape=tuple(out)...  991 us

profile of v3, /device:TPU:0, one launch (start us, length us, event | category | flops | bytes accessed | tf_op | source)
XLA Modules:
  0.0 1002.4 jit_solution(17686502252281262283)
XLA Ops:
  1.3 991.4 %step.1 = (bf16[512,3584]{1,0:T(8,128)(2,1)}, bf16[16384,256]{1,0:T(8,128)(2,1)}, bf16[8192,256]{1,0:T(8,128)(2,1)}, f32[8,2,256,512]{3,2,1,0:T(8,128)}, bf16[2,...) custom-call(s32[1]{0:T(128)S(6)} %copy.25.scal, ...), custom_call_target="tpu_custom_call" | custom-call | tf_op jit(solution)/shard_map/step/pallas_call | solution.py:906
  992.7 9.6 copy_out.1

commit v4 on v2

--- a/solution.py
+++ b/solution.py
@@ -20,7 +20,7 @@
 SLOTS = 5
 ROLL_ROWS = 256
 ROLL_SLOTS = 4
-EARLY = 2
+EARLY = 7
 LOWEST = -3.3e38
 VMEM_LIMIT = 67_043_328
 BF16 = jnp.bfloat16
@@ -248,12 +248,12 @@
     def scores(c, i, g, new, at):
         return score_tile(q_s[here(q_row(c, g, i), tall), :], tile_of(g, new, at, 0))
 
-    def row_blocks(body):
+    def row_blocks(body, first=0, last=rows):
         def one(n, carry):
             body(pl.ds(pl.multiple_of(n * ROW_BLOCK, ROW_BLOCK), ROW_BLOCK), n * ROW_BLOCK)
             return carry
 
-        lax.fori_loop(0, rows // ROW_BLOCK, one, 0)
+        lax.fori_loop(first // ROW_BLOCK, last // ROW_BLOCK, one, 0)
 
     def q_move(c, out):
         inner, outer = q_s.at[here(lax.rem(c, PAIR) * q_rows, q_rows)], q_hbm.at[here(c * q_rows, q_rows)]
@@ -271,13 +271,13 @@
                  (wo, wo_peer.at[layer]), (up, up_peer.at[layer]), (down, down_peer.at[layer]))
         return [remote(src.at[layer], dst, p_send.at[layer, k], p_recv.at[layer, k], place.peer) for k, (src, dst) in list(enumerate(pairs))[some]]
 
-    def norm_into(layer, which, c, slot):
+    def norm_into(layer, which, c, slot, *span):
         gain, shift = one_row(norms.at[layer], which), one_row(norms.at[layer], which + 1)
 
         def body(at, _):
             xo_s[slot, at, :] = normalized(mid_s[c, at, :].astype(F32), gain, shift)
 
-        row_blocks(body)
+        row_blocks(body, *span)
 
     def slot_of(layer, ahead):
         return lambda c: lax.rem(c + (SLOTS - layer + ahead), SLOTS)
@@ -294,6 +294,13 @@
     def lead(layer, c):
         if layer == 0:
             h_loads[c].wait()
+        if layer == 0 and c == 0:
+            for k in range(PAIR):
+                norm_into(0, 0, c, spot[0](c), k * rows // PAIR, (k + 1) * rows // PAIR)
+                for kind in (k, 3 - k):
+                    gather1[0].copy(c, kind).start()
+            return
+        if layer == 0:
             norm_into(0, 0, c, spot[0](c))
         gather1[layer].start(c)
 
@@ -308,10 +315,11 @@
     def pick(k):
         return jnp.where(k == 0, 3, jnp.where(k == 3, 0, k))
 
-    def state_move(b, out):
+    def state_out(n, c, i):
+        return pltpu.make_async_copy(st_s.at[lax.rem(n, PAIR)], state.at[c * GROUP + i], st_sem.at[lax.rem(n, PAIR)])
+
+    def state_in(b):
         slot = lax.rem(b, PAIR)
-        if out:
-            return pltpu.make_async_copy(st_s.at[slot], state.at[b], st_sem.at[slot])
         return pltpu.make_async_copy(state.at[lax.div(b, GROUP) * GROUP + pick(lax.rem(b, GROUP))], st_s.at[slot], st_sem.at[slot])
 
     def project_phase(layer):
@@ -373,7 +381,7 @@
         wa_fetch(jnp.int32(1))
 
         def attend_old(c, i):
-            b = c * GROUP + i
+            b = c * (GROUP - 1) + i
             w = lax.rem(b, PAIR)
             j0 = position(c, i)
             diag = lax.div(j0, tile)
@@ -382,7 +390,7 @@
 
             @pl.when(b >= PAIR)
             def _():
-                state_move(b - PAIR, True).wait()
+                state_out(b - PAIR, c, i).wait()
 
             reset_state(st_s, w)
 
@@ -409,7 +417,7 @@
                 return carry
 
             lax.fori_loop(1, tiles, younger, 0)
-            state_move(b, True).start()
+            state_out(b, c, i).start()
 
         def one_pass(p, carry):
             c = jnp.minimum(p, last_chunk)
@@ -489,14 +497,17 @@
             def _():
                 early = lax.div(p, 2)
                 for g in range(PAIR):
-                    s_s[g] = scores(early, 0, g, False, lax.div(position(early, 0), tile) * tile)
+                    s_s[g] = scores(early, early, g, False, lax.div(position(early, early), tile) * tile)
 
                 @pl.when(p == 2)
                 def _():
                     gather.forward(3)
 
                 def one(i, inner):
-                    attend_old(early, i)
+                    @pl.when(i >= early)
+                    def _():
+                        attend_old(early, i)
+
                     return inner
 
                 lax.fori_loop(0, GROUP, one, 0)
@@ -511,24 +522,22 @@
                 q_move(2, True).wait()
                 q_move(0, False).start()
                 for b in range(PAIR):
-                    state_move(jnp.int32(GROUP * EARLY - PAIR + b), True).wait()
-                    state_move(jnp.int32(b), False).start()
+                    state_out(jnp.int32(EARLY - PAIR + b), 0, 0).wait()
+                for b in range(PAIR):
+                    state_in(jnp.int32(b)).start()
 
             return carry
 
         lax.fori_loop(0, n_passes, one_pass, 0)
-        q_move(last_chunk, True).wait()
-        q_move(1, False).start()
         whole_chunk = big_s.at[pl.ds(0, PAIR * GROUP * rows)]
         kv_all = [remote(whole_chunk, whole_chunk, kv_send.at[c], kv_recv.at[c], place.peer) for c in range(chunks)]
         for copy in kv_all:
             copy.wait_recv()
-        for copy in kv_all + [old_push]:
-            copy.wait_send()
         for c in range(chunks):
             gather.drain(c)
-
-    def block_phase(layer):
+        return kv_all + [old_push]
+
+    def block_phase(layer, sent):
         onward = layer + 1 < layers
         gather = Gather(place, xo_s, spot[layer], a2_send, a2_recv, rows)
         first = Scatter(place, xo_s, slot_of(layer, 1), land_s, r1_send, r1_recv, rows)
@@ -555,7 +564,7 @@
             i = pick(k)
             b = c * GROUP + k
             w = lax.rem(b, PAIR)
-            late = c >= EARLY
+            late = b >= EARLY
             j0 = position(c, i)
             diag = lax.div(j0, tile)
             count = jnp.where(late, tiles + 1, diag + 2)
@@ -570,7 +579,7 @@
 
             @pl.when(jnp.logical_not(late))
             def _():
-                state_move(b, False).wait()
+                state_in(b).wait()
 
             def step(n):
                 is_new, at = tile_at(diag, n)
@@ -613,9 +622,9 @@
                     n = PAIR * g + h
                     xo_s[slot, :rows, n * hd:(n + 1) * hd] = out[h * rows:(h + 1) * rows]
 
-            @pl.when(b + PAIR < GROUP * EARLY)
-            def _():
-                state_move(b + PAIR, False).start()
+            @pl.when(b + PAIR < EARLY)
+            def _():
+                state_in(b + PAIR).start()
 
             @pl.when(b == 0)
             def _():
@@ -662,6 +671,11 @@
 
                 attend(c, k)
 
+                @pl.when(jnp.logical_and(c == 0, k == 1))
+                def _():
+                    q_move(last_chunk, True).wait()
+                    q_move(1, False).start()
+
                 @pl.when(jnp.where(c == 0, k == 3, jnp.logical_and(c >= 2, k == 0)))
                 def _():
                     first.relay(jnp.maximum(c - 1, 0), c - 2)
@@ -681,6 +695,8 @@
             return carry
 
         lax.fori_loop(0, chunks, attend_chunk, 0)
+        for copy in sent:
+            copy.wait_send()
         if onward:
             raw_copy(layer + 1, 0).start()
         for copy in pushes(layer, slice(4, None)):
@@ -835,8 +851,7 @@
                 o_copy(c).wait()
 
     for layer in range(layers):
-        project_phase(layer)
-        block_phase(layer)
+        block_phase(layer, project_phase(layer))
     for copy in b_copies:
         copy.wait_send()
     for layer in range(layers):
@@ -850,7 +865,7 @@
     layers, window, hd = caches[0].shape
     ffn = w_up.shape[2]
     dims = (layers, chunks, rows, model, hd, window, ffn)
-    state = (GROUP * EARLY, PAIR, PAIR * rows, PAIR * LANES + hd)
+    state = (PAIR * GROUP, PAIR, PAIR * rows, PAIR * LANES + hd)
     out = [tokens.shape, (layers * PAIR * window, hd), (chunks * PAIR * GROUP * PAIR * rows, hd), (layers, model, GROUP * hd), w_o.shape, w_up.shape, w_down.shape]
     out = [jax.ShapeDtypeStruct(o, BF16) for o in out]
     out.insert(3, jax.ShapeDtypeStruct(state, F32))

time: 997 us -> 991 us (level)
  no operation moved by 1% of the time
where the time goes in v4:
time: 991 us; the launch traced here: 990 us
  Pallas kernels  989 us (100%)
    pallas_call x1, Pallas kernels, run_step(): pl.pallas_call(functools.partial(step_kernel, dims), out_shape=tuple(out)...  979 us

profile of v4, /device:TPU:0, one launch (start us, length us, event | category | flops | bytes accessed | tf_op | source)
XLA Modules:
  0.0 990.3 jit_solution(18310517318525410972)
XLA Ops:
  1.3 979.2 %step.1 = (bf16[512,3584]{1,0:T(8,128)(2,1)}, bf16[16384,256]{1,0:T(8,128)(2,1)}, bf16[8192,256]{1,0:T(8,128)(2,1)}, f32[8,2,256,512]{3,2,1,0:T(8,128)}, bf16[2,...) custom-call(s32[1]{0:T(128)S(6)} %copy.25.scal, ...), custom_call_target="tpu_custom_call" | custom-call | tf_op jit(solution)/shard_map/step/pallas_call | solution.py:873
  980.5 9.6 copy_out.1

commit v5 on v4

--- a/solution.py
+++ b/solution.py
@@ -77,9 +77,11 @@
         st_s[w, g, :, LANES:] = jnp.zeros((st_s.shape[2], st_s.shape[3] - LANES), F32)
 
 
-def flash_step(st_s, w, s_s, scale, mask, values, next_scores):
+def flash_step(st_s, w, s_s, scale, mask, values, next_scores, width=KEY_TILE):
     for g in range(PAIR):
-        s = jnp.where(mask, s_s[g] * scale, -jnp.inf)
+        s = s_s[g, :, :width] * scale
+        if mask is not None:
+            s = jnp.where(mask, s, -jnp.inf)
         s_next = next_scores(g)
         m_prev = st_s[w, g, :, 0:LANES]
         m_next = jnp.maximum(m_prev, jnp.max(s, axis=1, keepdims=True))
@@ -92,7 +94,7 @@
         st_s[w, g, :, 0:LANES] = m_next
         mixed = jnp.dot(e.astype(BF16), values(g), preferred_element_type=F32)
         st_s[w, g, :, 2 * LANES:] = st_s[w, g, :, 2 * LANES:] * jnp.concatenate([alpha] * (mixed.shape[1] // LANES), axis=1) + mixed
-        s_s[g] = s_next
+        s_s[g, :, :s_next.shape[1]] = s_next
 
 
 def score_tile(queries, keys):
@@ -350,6 +352,8 @@
             at = position(c, i)
             return remote(big_s.at[here(region(g, True) + at, rows)], big_s.at[here(region(1 - g, True) + at, rows)], kv_send.at[c], kv_recv.at[c], place.peer)
 
+        whole_chunk = big_s.at[pl.ds(0, PAIR * GROUP * rows)]
+        kv_all = [remote(whole_chunk, whole_chunk, kv_send.at[c], kv_recv.at[c], place.peer) for c in range(chunks)]
         wa_fetch(jnp.int32(0))
         for copy in table_copies(0):
             copy.start()
@@ -526,13 +530,38 @@
                 for b in range(PAIR):
                     state_in(jnp.int32(b)).start()
 
+            @pl.when(p == 3)
+            def _():
+                for copy in kv_all[:3]:
+                    copy.wait_recv()
+                q_move(0, False).wait()
+                state_in(jnp.int32(0)).wait()
+                diag = lax.div(position(0, 3), tile)
+                width = 3 * rows
+
+                def keys(g, t, kv):
+                    return big_s[here(region(g, True) + t * tile, width), kv * hd:(kv + 1) * hd]
+
+                def score(g, t):
+                    return score_tile(q_s[here(q_row(0, g, 3), tall), :], keys(g, t, 0))
+
+                for g in range(PAIR):
+                    s_s[g, :, :width] = score(g, 0)
+
+                def earlier(t, inner):
+                    @pl.when(t < diag)
+                    def _():
+                        after = jnp.minimum(t + 1, tiles - 1)
+                        flash_step(st_s, 0, s_s, scale, None, lambda g: keys(g, t, 1), lambda g: score(g, after), width)
+
+                    return inner
+
+                lax.fori_loop(0, tiles - 1, earlier, 0)
+
             return carry
 
         lax.fori_loop(0, n_passes, one_pass, 0)
-        whole_chunk = big_s.at[pl.ds(0, PAIR * GROUP * rows)]
-        kv_all = [remote(whole_chunk, whole_chunk, kv_send.at[c], kv_recv.at[c], place.peer) for c in range(chunks)]
-        for copy in kv_all:
-            copy.wait_recv()
+        kv_all[3].wait_recv()
         for c in range(chunks):
             gather.drain(c)
         return kv_all + [old_push]
@@ -556,7 +585,6 @@
             t = jnp.where(n < 2, diag, jnp.where(is_new, n - 2, n - 1))
             return is_new, t * tile
 
-        q_move(jnp.int32(0), False).wait()
         for g in range(PAIR):
             s_s[g] = scores(jnp.int32(0), 3, g, True, lax.div(position(0, 3), tile) * tile)
 
@@ -567,7 +595,7 @@
             late = b >= EARLY
             j0 = position(c, i)
             diag = lax.div(j0, tile)
-            count = jnp.where(late, tiles + 1, diag + 2)
+            count = jnp.where(b == 0, 2, jnp.where(late, tiles + 1, diag + 2))
             end = k == 3
             c_next = jnp.minimum(jnp.where(end, c + 1, c), last_chunk)
             i_next = pick(jnp.where(end, 0, k + 1))
@@ -577,7 +605,7 @@
             def _():
                 reset_state(st_s, w)
 
-            @pl.when(jnp.logical_not(late))
+            @pl.when(jnp.logical_and(jnp.logical_not(late), b > 0))
             def _():
                 state_in(b).wait()
 
@@ -605,6 +633,22 @@
             @pl.when(late)
             def _():
                 step(1)
+
+            def last_keys(u, carry):
+                @pl.when(jnp.logical_and(b == 0, u * GROUP < diag))
+                def _():
+                    def gathered(g, kv):
+                        cols = slice(kv * hd, (kv + 1) * hd)
+                        return jnp.concatenate([big_s[here(region(g, True) + (u * GROUP + n + 1) * tile - rows, rows), cols] for n in range(GROUP)], axis=0)
+
+                    for g in range(PAIR):
+                        s_s[g] = score_tile(q_s[here(q_row(c, g, i), tall), :], gathered(g, 0))
+                    seen = lax.broadcasted_iota(jnp.int32, (1, tile), 1) < (diag - u * GROUP) * rows
+                    flash_step(st_s, w, s_s, scale, seen, lambda g: gathered(g, 1), lambda g: scores(c_next, i_next, g, True, next_at))
+
+                return carry
+
+            lax.fori_loop(0, PAIR, last_keys, 0)
 
             def further(n, carry):
                 @pl.when(n < count)

time: 991 us -> 990 us (level)
  no operation moved by 1% of the time
where the time goes in v5:
time: 990 us
  Pallas kernels  988 us (100%)
    pallas_call x1, Pallas kernels, run_step(): pl.pallas_call(functools.partial(step_kernel, dims), out_shape=tuple(out)...  979 us

profile of v5, /device:TPU:0, one launch (start us, length us, event | category | flops | bytes accessed | tf_op | source)
XLA Modules:
  0.0 989.6 jit_solution(2973067283706908494)
XLA Ops:
  1.3 978.5 %step.1 = (bf16[512,3584]{1,0:T(8,128)(2,1)}, bf16[16384,256]{1,0:T(8,128)(2,1)}, bf16[8192,256]{1,0:T(8,128)(2,1)}, f32[8,2,256,512]{3,2,1,0:T(8,128)}, bf16[2,...) custom-call(s32[1]{0:T(128)S(6)} %copy.25.scal, ...), custom_call_target="tpu_custom_call" | custom-call | tf_op jit(solution)/shard_map/step/pallas_call | solution.py:917
  979.8 9.6 copy_out.1

commit v6 on v5

--- a/solution.py
+++ b/solution.py
@@ -13,7 +13,7 @@
 KEY_TILE = 512
 LANES = 128
 WIDE = 512
-ROW_BLOCK = 16
+ROW_BLOCK = 32
 PAIR = 2
 GROUP = 4
 WEIGHT_SLOTS = 3
@@ -116,11 +116,10 @@
         yb = self.yb + lax.div(i, 2) * (1 - 2 * self.yb)
         return yb * 2 + xb
 
-    def barrier(self, others):
+    def arrive(self, others):
         sem = pltpu.get_barrier_semaphore()
         for other in others:
             pl.semaphore_signal(sem, inc=1, device_id={'tp': other}, device_id_type=MESH)
-        pl.semaphore_wait(sem, len(others))
 
 
 def remote(src, dst, send_sem, recv_sem, other):
@@ -288,10 +287,11 @@
     spare = [(SLOTS - 1 - layer) % SLOTS for layer in range(layers)]
     gather1 = [Gather(place, xo_s, spot[layer], a1_send, a1_recv, rows) for layer in range(layers)]
     h_loads = [pltpu.make_async_copy(tokens.at[pl.ds(c * rows, rows)], mid_s.at[c], h_sem.at[c]) for c in range(chunks)]
+    near = (place.x, place.y, place.peer)
+    place.arrive(near)
     for copy in h_loads:
         copy.start()
     raw_copy(0, 0).start()
-    place.barrier((place.x, place.y, place.peer))
 
     def lead(layer, c):
         if layer == 0:
@@ -299,6 +299,8 @@
         if layer == 0 and c == 0:
             for k in range(PAIR):
                 norm_into(0, 0, c, spot[0](c), k * rows // PAIR, (k + 1) * rows // PAIR)
+                if k == 0:
+                    pl.semaphore_wait(pltpu.get_barrier_semaphore(), len(near))
                 for kind in (k, 3 - k):
                     gather1[0].copy(c, kind).start()
             return
@@ -866,8 +868,10 @@
         def o_copy(c):
             return pltpu.make_async_copy(mid_s.at[c], h_out.at[here(c * rows, rows)], h_sem.at[c])
 
-        second.relay(2, 1 if onward else None)
-        second.relay(3, 2 if onward else None)
+        second.relay(2, None)
+        second.relay(3, None)
+        if onward:
+            second.drain(1)
 
         def close(c, carry):
             second.finish(c)
@@ -888,6 +892,7 @@
 
         lax.fori_loop(0, chunks, close, 0)
         if onward:
+            second.drain(2)
             second.drain(last_chunk)
         else:
             for c in range(chunks):

time: 990 us -> 990 us (level)
  no operation moved by 1% of the time
where the time goes in v6:
time: 990 us; the launch traced here: 989 us
  Pallas kernels  988 us (100%)
    pallas_call x1, Pallas kernels, run_step(): pl.pallas_call(functools.partial(step_kernel, dims), out_shape=tuple(out)...  978 us

profile of v6, /device:TPU:0, one launch (start us, length us, event | category | flops | bytes accessed | tf_op | source)
XLA Modules:
  0.0 989.5 jit_solution(5620063453391479256)
XLA Ops:
  1.3 978.4 %step.1 = (bf16[512,3584]{1,0:T(8,128)(2,1)}, bf16[16384,256]{1,0:T(8,128)(2,1)}, bf16[8192,256]{1,0:T(8,128)(2,1)}, f32[8,2,256,512]{3,2,1,0:T(8,128)}, bf16[2,...) custom-call(s32[1]{0:T(128)S(6)} %copy.25.scal, ...), custom_call_target="tpu_custom_call" | custom-call | tf_op jit(solution)/shard_map/step/pallas_call | solution.py:922
  979.7 9.6 copy_out.1

commit v7 on v6

--- a/solution.py
+++ b/solution.py
@@ -20,7 +20,7 @@
 SLOTS = 5
 ROLL_ROWS = 256
 ROLL_SLOTS = 4
-EARLY = 7
+EARLY = 6
 LOWEST = -3.3e38
 VMEM_LIMIT = 67_043_328
 BF16 = jnp.bfloat16
@@ -387,11 +387,11 @@
         wa_fetch(jnp.int32(1))
 
         def attend_old(c, i):
-            b = c * (GROUP - 1) + i
+            b = jnp.where(c == 0, i, GROUP + lax.div(i, 2))
             w = lax.rem(b, PAIR)
             j0 = position(c, i)
             diag = lax.div(j0, tile)
-            i_next = jnp.minimum(i + 1, GROUP - 1)
+            i_next = jnp.where(c == 0, jnp.minimum(i + 1, GROUP - 1), GROUP - 1)
             diag_next = lax.div(position(c, i_next), tile)
 
             @pl.when(b >= PAIR)
@@ -510,7 +510,7 @@
                     gather.forward(3)
 
                 def one(i, inner):
-                    @pl.when(i >= early)
+                    @pl.when(jnp.logical_or(early == 0, lax.rem(i, 2) == 1))
                     def _():
                         attend_old(early, i)
 

time: 990 us -> 989 us (level)
  no operation moved by 1% of the time
where the time goes in v7:
time: 989 us
  Pallas kernels  987 us (100%)
    pallas_call x1, Pallas kernels, run_step(): pl.pallas_call(functools.partial(step_kernel, dims), out_shape=tuple(out)...  978 us

profile of v7, /device:TPU:0, one launch (start us, length us, event | category | flops | bytes accessed | tf_op | source)
XLA Modules:
  0.0 988.9 jit_solution(4286727893143082196)
XLA Ops:
  1.3 977.8 %step.1 = (bf16[512,3584]{1,0:T(8,128)(2,1)}, bf16[16384,256]{1,0:T(8,128)(2,1)}, bf16[8192,256]{1,0:T(8,128)(2,1)}, f32[8,2,256,512]{3,2,1,0:T(8,128)}, bf16[2,...) custom-call(s32[1]{0:T(128)S(6)} %copy.25.scal, ...), custom_call_target="tpu_custom_call" | custom-call | tf_op jit(solution)/shard_map/step/pallas_call | solution.py:922
  979.1 9.6 copy_out.1

commit v8 on v7

--- a/solution.py
+++ b/solution.py
@@ -547,18 +547,20 @@
                 def score(g, t):
                     return score_tile(q_s[here(q_row(0, g, 3), tall), :], keys(g, t, 0))
 
+                row = lax.rem(lax.broadcasted_iota(jnp.int32, (tall, 1), 0), rows) + position(0, 3)
+                col = lax.broadcasted_iota(jnp.int32, (1, width), 1)
                 for g in range(PAIR):
                     s_s[g, :, :width] = score(g, 0)
 
                 def earlier(t, inner):
-                    @pl.when(t < diag)
+                    @pl.when(t <= diag)
                     def _():
                         after = jnp.minimum(t + 1, tiles - 1)
-                        flash_step(st_s, 0, s_s, scale, None, lambda g: keys(g, t, 1), lambda g: score(g, after), width)
+                        flash_step(st_s, 0, s_s, scale, col + t * tile <= row, lambda g: keys(g, t, 1), lambda g: score(g, after), width)
 
                     return inner
 
-                lax.fori_loop(0, tiles - 1, earlier, 0)
+                lax.fori_loop(0, tiles, earlier, 0)
 
             return carry
 
@@ -587,8 +589,10 @@
             t = jnp.where(n < 2, diag, jnp.where(is_new, n - 2, n - 1))
             return is_new, t * tile
 
-        for g in range(PAIR):
-            s_s[g] = scores(jnp.int32(0), 3, g, True, lax.div(position(0, 3), tile) * tile)
+        @pl.when(lax.div(position(0, 3), tile) == 0)
+        def _():
+            for g in range(PAIR):
+                s_s[g] = scores(jnp.int32(0), 1, g, True, lax.div(position(0, 1), tile) * tile)
 
         def attend(c, k):
             i = pick(k)
@@ -597,7 +601,7 @@
             late = b >= EARLY
             j0 = position(c, i)
             diag = lax.div(j0, tile)
-            count = jnp.where(b == 0, 2, jnp.where(late, tiles + 1, diag + 2))
+            count = jnp.where(b == 0, 0, jnp.where(late, tiles + 1, diag + 2))
             end = k == 3
             c_next = jnp.minimum(jnp.where(end, c + 1, c), last_chunk)
             i_next = pick(jnp.where(end, 0, k + 1))
@@ -630,7 +634,9 @@
                     mask = col > jnp.maximum(row, floor)
                 flash_step(st_s, w, s_s, scale, mask, lambda g: tile_of(g, is_new, at, 1), lambda g: scores(nc, ni, g, new_next, at_next))
 
-            step(0)
+            @pl.when(b > 0)
+            def _():
+                step(0)
 
             @pl.when(late)
             def _():

time: 989 us -> 990 us (level)
  no operation moved by 1% of the time
where the time goes in v8:
time: 990 us
  Pallas kernels  988 us (100%)
    pallas_call x1, Pallas kernels, run_step(): pl.pallas_call(functools.partial(step_kernel, dims), out_shape=tuple(out)...  978 us

profile of v8, /device:TPU:0, one launch (start us, length us, event | category | flops | bytes accessed | tf_op | source)
XLA Modules:
  0.0 989.5 jit_solution(5218490094112485884)
XLA Ops:
  1.3 978.5 %step.1 = (bf16[512,3584]{1,0:T(8,128)(2,1)}, bf16[16384,256]{1,0:T(8,128)(2,1)}, bf16[8192,256]{1,0:T(8,128)(2,1)}, f32[8,2,256,512]{3,2,1,0:T(8,128)}, bf16[2,...) custom-call(s32[1]{0:T(128)S(6)} %copy.25.scal, ...), custom_call_target="tpu_custom_call" | custom-call | tf_op jit(solution)/shard_map/step/pallas_call | solution.py:928
  979.8 9.6 copy_out.1
